TPU v7x, 128 devices: a whole 4x4x4 slice. The times are simulated.
128 devices in a mesh: row: 8 (over x, core), col: 4 (over z), depth: 4 (over y).
Axes of the slice: x: 4, y: 4, z: 4, core: 2. Of those that a mesh axis runs over, the one named last changes fastest.
Arguments:
- trailing: float32 [8192, 8192], P('row', 'col'), may hold values from -6 to 6
- panel: bfloat16 [8192, 4096], P('row', 'col'), may hold values from -0.75 to 0.75
- inverse_factor: bfloat16 [4096, 4096], P('depth', 'col'), may hold values from -0.09375 to 0.09375
- block_inverse: float32 [8192, 512], P('row'), may hold values from -0.25 to 0.25
- guess: float32 [8192, 128], P(('col', 'depth')), may hold values from -0.0625 to 0.0625
- target: float32 [8192, 128], P('row'), may hold values from -6 to 6
Outputs:
- updated: float32 [8192, 8192], P('row', ('col', 'depth'))
- correction: float32 [8192, 128], P('row')
- residual_rms: float32 [1], replicated
All inputs are finite; a program needn't handle non-finite values.
Results may differ from a plain program's by a relative error of at most 0.00036.
Values may be sent and summed in bfloat16 or wider, within the bound.
No kernel may reach another device: no remote copies, remote signals or barrier semaphores. Data moves between devices by JAX's collectives and lax.ppermute only.
A program may use at most 128 MiB of HBM per device.

v0:
```python
import jax
import jax.numpy as jnp
from jax import lax
from jax.experimental import pallas as pl
from jax.experimental.pallas import tpu as pltpu
from jax.sharding import PartitionSpec as P


N = 8192
BS = 512
R = 128
F32 = jnp.float32
BF16 = jnp.bfloat16
PLANE = ("col", "depth")
ALL = ("row", "col", "depth")


def ring(size, step):
    return [(i, (i + step) % size) for i in range(size)]


def gather_ring(block, axis, step, size):
    half = block.shape[0] // 2
    prev = lax.ppermute(block, axis, ring(size, step))
    succ = lax.ppermute(block, axis, ring(size, -step))
    far_a = lax.ppermute(prev[:half], axis, ring(size, step))
    far_b = lax.ppermute(succ[half:], axis, ring(size, -step))
    return block, prev, succ, far_a, far_b


def gather_direct(block, axis, step, size):
    prev = lax.ppermute(block, axis, ring(size, step))
    succ = lax.ppermute(block, axis, ring(size, -step))
    far = lax.ppermute(block, axis, ring(size, 2 * step))
    return block, prev, succ, far


def joined(parts):
    return jnp.concatenate(parts, axis=0)


def dot_t(a, b):
    return lax.dot_general(a, b, (((1,), (1,)), ((), ())), preferred_element_type=F32)


def first_kernel(idx, panel, inverse, lower, fb, sb, rows, raw, sems):
    copies = [
        pltpu.make_async_copy(inverse.at[256 * i : 256 * i + 256], raw.at[256 * i : 256 * i + 256], sems.at[i])
        for i in range(4)
    ]
    for i, k in enumerate((3, 2)):
        start = pl.multiple_of(idx[k] + 128, 128)
        copies.append(
            pltpu.make_async_copy(panel.at[pl.ds(start, 128)], rows.at[128 * i : 128 * i + 128], sems.at[4 + i])
        )
    for copy in copies:
        copy.start()
    for i in range(4):
        copies[i].wait()
        block = slice(256 * i, 256 * i + 256)
        shape = (256, 1024)
        k_index = idx[4] + 256 * i + lax.broadcasted_iota(jnp.int32, shape, 0)
        j_index = idx[5] + lax.broadcasted_iota(jnp.int32, shape, 1)
        lower[block, :] = jnp.where(k_index >= j_index, raw[block, :].astype(F32), 0.0).astype(BF16)
    copies[4].wait()
    copies[5].wait()
    both = dot_t(rows[...], lower[...])
    fb[...] = both[:128]
    sb[...] = both[128:]


def second_kernel(idx, panel, lower, fa, pb, pa, sa):
    far = panel[pl.ds(pl.multiple_of(idx[3], 128), 128), :]
    prev = panel[pl.ds(pl.multiple_of(idx[1], 128), 256), :]
    succ = panel[pl.ds(pl.multiple_of(idx[2], 128), 128), :]
    out = dot_t(jnp.concatenate([far, prev, succ], axis=0), lower[...])
    fa[...] = out[:128]
    pa[...] = out[128:256]
    pb[...] = out[256:384]
    sa[...] = out[384:]


def own_kernel(idx, panel, lower, top, bottom):
    out = dot_t(panel[pl.ds(pl.multiple_of(idx[0], 128), 256), :], lower[...])
    top[...] = out[:128]
    bottom[...] = out[128:]


def factor_share(panel, inverse_factor, idx):
    piece = jax.ShapeDtypeStruct((128, 1024), F32)
    square = jax.ShapeDtypeStruct((1024, 1024), BF16)
    lower, fb, sb = on_core(
        first_kernel,
        (square, piece, piece),
        (idx, panel, inverse_factor),
        2**29,
        scratch=(
            pltpu.VMEM((256, 1024), BF16),
            pltpu.VMEM((1024, 1024), BF16),
            pltpu.SemaphoreType.DMA((6,)),
        ),
        whole=2,
    )
    s_b = lax.ppermute(sb, "col", ring(4, 1))
    far_b = lax.ppermute(fb, "col", ring(4, -1))
    fa, pb, pa, sa = on_core(second_kernel, (piece,) * 4, (idx, panel, lower), 2**30)
    far_a = lax.ppermute(fa, "col", ring(4, 1))
    p_b = lax.ppermute(pb + far_b, "col", ring(4, -1))
    p_a = lax.ppermute(pa, "col", ring(4, -1))
    s_a = lax.ppermute(sa + far_a, "col", ring(4, 1))
    own_top, own_bottom = on_core(own_kernel, (piece, piece), (idx, panel, lower), 2**29)
    top = own_top + s_a + p_a
    bottom = own_bottom + s_b + p_b
    return top.astype(BF16), bottom.astype(BF16)


def turned():
    pairs = []
    for r in range(8):
        for c in range(4):
            for d in range(4):
                x, core = divmod(r, 2)
                depth = 2 * core + c // 2
                row = 2 * ((d + 2 * core + x) % 4) + c % 2
                pairs.append(((r * 4 + c) * 4 + d, (row * 4 + x) * 4 + depth))
    return pairs


def three(x):
    high = x.astype(BF16)
    rest = x - high.astype(F32)
    mid = rest.astype(BF16)
    return high, mid, (rest - mid.astype(F32)).astype(BF16)


def full_dot(a, b):
    high, mid, low = three(a)
    b_high, b_mid, b_low = three(b)
    first = jnp.dot(high, jnp.concatenate([b_high, b_mid], axis=1), preferred_element_type=F32)
    second = jnp.dot(mid, jnp.concatenate([b_high, b_mid], axis=1), preferred_element_type=F32)
    third = jnp.dot(high, b_low, preferred_element_type=F32) + jnp.dot(low, b_high, preferred_element_type=F32)
    return first[:, :R] + ((first[:, R:] + second[:, :R]) + (second[:, R:] + third))


def early_kernel(
    idx, guess, z_all, zor, zol, zr, zl, yd, yr, yl, bt, bb, ct, cb, trailing,
    acc, applied, b_all, z_in, y_in, b_in, mine, sems,
):
    b_copies = [pltpu.make_async_copy(b, b_in.at[i], sems.at[i]) for i, b in enumerate((bt, bb, ct, cb))]
    y_copies = [pltpu.make_async_copy(y, y_in.at[i], sems.at[4 + i]) for i, y in enumerate((yd, yr, yl))]
    z_copies = [
        [pltpu.make_async_copy(z_all, z_in.at[0], sems.at[7])],
        [
            pltpu.make_async_copy(zor, z_in.at[1, :128], sems.at[8]),
            pltpu.make_async_copy(zr, z_in.at[1, 128:], sems.at[9]),
        ],
        [
            pltpu.make_async_copy(zol, z_in.at[2, :128], sems.at[10]),
            pltpu.make_async_copy(zl, z_in.at[2, 128:], sems.at[11]),
        ],
    ]
    columns = pl.ds(pl.multiple_of(idx[10] * 512, 512), 512)
    last = pltpu.make_async_copy(trailing.at[:, columns], mine, sems.at[12])
    for copy in b_copies + z_copies[0] + y_copies + z_copies[1] + z_copies[2] + [last]:
        copy.start()
    for copy in b_copies:
        copy.wait()
    z_total = y_total = None
    for t in range(4):
        b = jnp.concatenate([b_in[i, idx[4 + t]] for i in range(4)], axis=0)
        b_all[512 * t : 512 * t + 512, :] = b
        if t < 3:
            for copy in z_copies[t]:
                copy.wait()
            part = dot_t(z_in[t], b)
            z_total = part if t == 0 else z_total + part
        if t == 0:
            for copy in y_copies:
                copy.wait()
        y = jnp.concatenate([y_in[i, 128 * t : 128 * t + 128, :] for i in range(3)], axis=0)
        part = dot_t(y, b)
        y_total = part if t == 0 else y_total + part
    last.wait()
    for h in range(2):
        cols = pl.ds(pl.multiple_of(idx[8 + h] * 256, 256), 256)
        half = slice(256 * h, 256 * h + 256)
        for i in range(4):
            rows = pl.ds(pl.multiple_of(idx[i], 128), 128)
            acc[rows, cols] = mine[rows, cols] - z_total[128 * i : 128 * i + 128, half]
            rows = pl.ds(pl.multiple_of(idx[i] + 128, 128), 128)
            if i < 3:
                acc[rows, cols] = mine[rows, cols] - y_total[128 * i : 128 * i + 128, half]
            else:
                acc[rows, cols] = mine[rows, cols]
    applied[...] = full_dot(acc[...], guess[...])


def late_kernel(idx, za, zb, ya, yb, b_all, acc, early, guess, updated, applied, part):
    z = jnp.concatenate([za[...], zb[...], yb[128:, :]], axis=0)
    z = dot_t(z, b_all[1536:, :])
    y = z[512:]
    for t, block in enumerate((ya[:128, :], ya[128:, :], yb[:128, :])):
        y = y + dot_t(block, b_all[512 * t : 512 * t + 512, :])
    for h in range(2):
        cols = pl.ds(pl.multiple_of(idx[8 + h] * 256, 256), 256)
        half = slice(256 * h, 256 * h + 256)
        part[:512, cols] = z[:512, half]
        part[512:, cols] = y[:, half]
    last = full_dot(part[...], guess[...])
    updated[...] = acc[...]
    applied[...] = early[...]
    for i in range(5):
        start = idx[i] if i < 4 else idx[3] + 128
        rows = pl.ds(pl.multiple_of(start, 128), 128)
        mine = slice(128 * i, 128 * i + 128)
        updated[rows, :] = acc[rows, :] - part[mine, :]
        applied[rows, :] = early[rows, :] - last[mine]


def on_core(kernel, outs, inputs, flops, vmem_mib=24, scratch=(), whole=0):
    size = sum(a.size * a.dtype.itemsize for a in inputs)
    vmem = pl.BlockSpec(memory_space=pltpu.VMEM)
    smem = pl.BlockSpec(memory_space=pltpu.SMEM)
    away = pl.BlockSpec(memory_space=pltpu.HBM)
    return pl.pallas_call(
        kernel,
        out_shape=outs,
        in_specs=[smem] + [vmem] * (len(inputs) - 1 - whole) + [away] * whole,
        out_specs=jax.tree.map(lambda _: vmem, outs),
        scratch_shapes=list(scratch),
        cost_estimate=pl.CostEstimate(flops=flops, bytes_accessed=size, transcendentals=0),
        compiler_params=pltpu.CompilerParams(vmem_limit_bytes=vmem_mib * 1024 * 1024),
    )(*inputs)


def pack_kernel(own, prev, succ, far, out):
    for i, part in enumerate((own, prev, succ, far)):
        out[i] = part[...]


def pack(parts):
    vmem = pl.BlockSpec(memory_space=pltpu.VMEM)
    return pl.pallas_call(
        pack_kernel,
        out_shape=jax.ShapeDtypeStruct((4, *parts[0].shape), parts[0].dtype),
        in_specs=[vmem] * 4,
        out_specs=vmem,
        cost_estimate=pl.CostEstimate(flops=2**20, bytes_accessed=2**22, transcendentals=0),
        compiler_params=pltpu.CompilerParams(vmem_limit_bytes=8 * 1024 * 1024),
    )(*parts)


def gram_kernel(inverse, gram):
    keep = lax.broadcasted_iota(jnp.int32, (BS, BS), 0) >= lax.broadcasted_iota(jnp.int32, (BS, BS), 1)
    for i in range(2):
        g = jnp.where(keep, inverse[BS * i : BS * i + BS, :], 0.0)
        gram[i] = lax.dot_general(
            g, g, (((0,), (0,)), ((), ())), precision=lax.Precision.HIGHEST, preferred_element_type=F32
        )


def correct_kernel(gram, residual, correction):
    for i in range(2):
        rows = slice(BS * i, BS * i + BS)
        correction[rows, :] = full_dot(gram[i], residual[rows, :])


def body(trailing, panel, inverse_factor, block_inverse, guess, target):
    row_id = lax.axis_index("row")
    col_id = lax.axis_index("col")
    depth_id = lax.axis_index("depth")
    x_id, core_id = row_id // 2, row_id % 2
    starts = [256 * ((col_id + k) % 4) for k in (0, 3, 1, 2)]
    at = jnp.stack(starts + [depth_id * 1024, col_id * 1024]).astype(jnp.int32)
    top, bottom = factor_share(panel, inverse_factor, at)

    gram = pl.pallas_call(
        gram_kernel,
        out_shape=jax.ShapeDtypeStruct((2, BS, BS), F32),
        cost_estimate=pl.CostEstimate(flops=2**32, bytes_accessed=2**22, transcendentals=0),
        compiler_params=pltpu.CompilerParams(vmem_limit_bytes=16 * 1024 * 1024),
    )(block_inverse)

    b_own, b_other = [], []
    for half in (top, bottom):
        line = lax.ppermute(half, ALL, turned())
        parts = gather_direct(line, "row", 2, 8)
        packed = pack(parts)
        b_own.append(packed)
        b_other.append(lax.ppermute(packed, "row", [(i, i ^ 1) for i in range(8)]))

    z_parts = gather_direct(top, "col", 1, 4)
    z_all = joined(z_parts)
    y_all = joined(gather_direct(bottom, "depth", 1, 4))
    z_own_r = lax.ppermute(top, "depth", ring(4, 1))
    z_own_l = lax.ppermute(top, "depth", ring(4, -1))
    z_rest = joined(z_parts[1:])
    zr = lax.ppermute(z_rest, "depth", ring(4, 1))
    zl = lax.ppermute(z_rest, "depth", ring(4, -1))
    za = lax.ppermute(joined([z_own_r, zr[:128]]), "depth", ring(4, 1))
    zb = lax.ppermute(zl[128:], "depth", ring(4, -1))
    yd, yr, yl, ya, yb = gather_ring(y_all, "col", 1, 4)

    offsets = [256 * ((col_id + k) % 4) for k in (0, 3, 1, 2)]
    places = []
    for k in (0, 3, 1, 2):
        dx = (depth_id + k + 2 * (depth_id // 2) + col_id - x_id) % 4
        places.append(jnp.where(dx == 0, 0, jnp.where(dx == 3, 1, dx + 1)))
    idx = jnp.stack(offsets + places + [core_id, 1 - core_id, depth_id]).astype(jnp.int32)

    tile = jax.ShapeDtypeStruct((1024, 512), F32)
    narrow = jax.ShapeDtypeStruct((1024, R), F32)
    acc, early, b_all = on_core(
        early_kernel,
        (tile, narrow, jax.ShapeDtypeStruct((2048, 1024), BF16)),
        (idx, guess, z_all, z_own_r, z_own_l, zr, zl, yd, yr, yl, *b_own, *b_other, trailing),
        2 * 512 * 1024 * (896 * 3 + 384),
        vmem_mib=40,
        scratch=(
            pltpu.VMEM((3, 512, 1024), BF16),
            pltpu.VMEM((3, 512, 1024), BF16),
            pltpu.VMEM((4, 4, 128, 1024), BF16),
            pltpu.VMEM((1024, 512), F32),
            pltpu.SemaphoreType.DMA((13,)),
        ),
        whole=13,
    )
    updated, applied = on_core(
        late_kernel,
        (tile, narrow),
        (idx, za, zb, ya, yb, b_all, acc, early, guess),
        2 * 512 * 1024 * 1024,
        scratch=(pltpu.VMEM((640, 512), F32),),
    )

    pieces = lax.all_to_all(applied.reshape(16, 64, R), PLANE, 0, 0, tiled=True)
    piece_id = col_id * 4 + depth_id
    part = lax.dynamic_slice_in_dim(target, piece_id * 64, 64, 0) - pieces.sum(axis=0)
    residual = lax.all_to_all(jnp.broadcast_to(part[None], (16, 64, R)), PLANE, 0, 0, tiled=True)
    residual = residual.reshape(1024, R)
    squares = jnp.sum(residual * residual)
    squares = lax.all_to_all(jnp.broadcast_to(squares, (8, 1, 1)), "row", 0, 0, tiled=True).sum(axis=0)
    residual_rms = jnp.sqrt(squares / (N * R))
    correction = pl.pallas_call(
        correct_kernel,
        out_shape=jax.ShapeDtypeStruct((1024, R), F32),
        cost_estimate=pl.CostEstimate(flops=2**30, bytes_accessed=2**22, transcendentals=0),
        compiler_params=pltpu.CompilerParams(vmem_limit_bytes=16 * 1024 * 1024),
    )(gram, residual)
    return (updated, correction, residual_rms.reshape(1))


def solution(mesh):
    placed = (
        P("row", "col"),
        P("row", "col"),
        P("depth", "col"),
        P("row", None),
        P(("col", "depth"), None),
        P("row", None),
    )
    return jax.shard_map(
        body,
        mesh=mesh,
        in_specs=placed,
        out_specs=(P("row", ("col", "depth")), P("row", None), P()),
        check_vma=False,
    )
```

profile of v0, /device:TPU:1, one launch (start us, length us, event | category | flops | bytes accessed | tf_op | source)
XLA Modules:
  0.0 220.2 jit_solution(12431655886122896010)
XLA Ops:
  7.8 2.5 %collective-permute-start = (f32[128,1024]{1,0:T(8,128)S(1)}, f32[128,1024]{1,0:T(8,128)S(1)}, u32[]{:S(2)}, u32[]{:S(2)}) collective-permute-start(f32[128,1024]{1,0:T(8,128)S(1)} %get-tuple-element.20), channel_id=1, source_target_pairs={{0,4},{4,8},{8,12},{12,0},{1,5},{5,9},{9,13},{13,1},{2,6},{6,10},{... | collective-permute-start | bytes 1572872 | tf_op jit(solution)/shard_map/ppermute | solution.py:107
  10.4 2.2 collective-permute-start.12
  13.9 10.2 %collective-permute-done = f32[128,1024]{1,0:T(8,128)S(1)} collective-permute-done((f32[128,1024]{1,0:T(8,128)S(1)}, f32[128,1024]{1,0:T(8,128)S(1)}, u32[]{:S(2)}, u32[]{:S(2)}) %collective-permute-start) | collective-permute-done | bytes 524320 | tf_op jit(solution)/shard_map/ppermute | solution.py:107
  25.0 2.1 collective-permute-start.13
  28.4 6.0 %collective-permute-done.2 = f32[128,1024]{1,0:T(8,128)S(1)} collective-permute-done((f32[128,1024]{1,0:T(8,128)S(1)}, f32[128,1024]{1,0:T(8,128)S(1)}, u32[]{:S(2)}, u32[]{:S(2)}) %collective-permute-start.2) | collective-permute-done | bytes 524320 | tf_op jit(solution)/shard_map/ppermute | solution.py:109
  34.5 3.2 %collective-permute-done.1 = f32[128,1024]{1,0:T(8,128)S(1)} collective-permute-done((f32[128,1024]{1,0:T(8,128)S(1)}, f32[128,1024]{1,0:T(8,128)S(1)}, u32[]{:S(2)}, u32[]{:S(2)}) %collective-permute-start.1) | collective-permute-done | bytes 524320 | tf_op jit(solution)/shard_map/ppermute | solution.py:110
  37.8 11.0 %collective-permute-start.22 = (bf16[128,1024]{1,0:T(8,128)(2,1)S(1)}, bf16[128,1024]{1,0:T(8,128)(2,1)S(1)}, u32[]{:S(2)}, u32[]{:S(2)}) collective-permute-start(bf16[128,1024]{1,0:T(8,128)(2,1)S(1)} %add_convert_fusion.1), channel_id=1, source_target_pairs={{0,0},{1,32},{2,64},{3,96},{4,16},{5,48},{6,80},{7,112},{8,1},{9,3... | collective-permute-start | bytes 786440 | tf_op jit(solution)/shard_map/ppermute | solution.py:286
  48.9 2.7 %collective-permute-start.5 = (bf16[128,1024]{1,0:T(8,128)(2,1)S(1)}, bf16[128,1024]{1,0:T(8,128)(2,1)S(1)}, u32[]{:S(2)}, u32[]{:S(2)}) collective-permute-start(bf16[128,1024]{1,0:T(8,128)(2,1)S(1)} %add_convert_fusion.1), channel_id=1, source_target_pairs={{0,12},{4,0},{8,4},{12,8},{1,13},{5,1},{9,5},{13,9},{2,14},{6,2},{... | collective-permute-start | bytes 786440 | tf_op jit(solution)/shard_map/ppermute | solution.py:33
  52.9 8.5 %collective-permute-start.26 = (bf16[128,1024]{1,0:T(8,128)(2,1)S(1)}, bf16[128,1024]{1,0:T(8,128)(2,1)S(1)}, u32[]{:S(2)}, u32[]{:S(2)}) collective-permute-start(bf16[128,1024]{1,0:T(8,128)(2,1)S(1)} %add_convert_fusion), channel_id=1, source_target_pairs={{0,0},{1,32},{2,64},{3,96},{4,16},{5,48},{6,80},{7,112},{8,1},{9,3... | collective-permute-start | bytes 786440 | tf_op jit(solution)/shard_map/ppermute | solution.py:286
  61.6 3.9 %collective-permute-start.14 = (bf16[128,1024]{1,0:T(8,128)(2,1)S(1)}, bf16[128,1024]{1,0:T(8,128)(2,1)S(1)}, u32[]{:S(2)}, u32[]{:S(2)}) collective-permute-start(bf16[128,1024]{1,0:T(8,128)(2,1)S(1)} %add_convert_fusion), channel_id=1, source_target_pairs={{0,1},{1,2},{2,3},{3,0},{4,5},{5,6},{6,7},{7,4},{8,9},{9,10},{10,1... | collective-permute-start | bytes 786440 | tf_op jit(solution)/shard_map/ppermute | solution.py:32
  65.7 6.8 %collective-permute-done.6 = bf16[128,1024]{1,0:T(8,128)(2,1)S(1)} collective-permute-done((bf16[128,1024]{1,0:T(8,128)(2,1)S(1)}, bf16[128,1024]{1,0:T(8,128)(2,1)S(1)}, u32[]{:S(2)}, u32[]{:S(2)}) %collective-permute-start.6) | collective-permute-done | bytes 262176 | tf_op jit(solution)/shard_map/ppermute | solution.py:34
  79.2 19.2 %collective-permute-done.16 = bf16[128,1024]{1,0:T(8,128)(2,1)S(1)} collective-permute-done((bf16[128,1024]{1,0:T(8,128)(2,1)S(1)}, bf16[128,1024]{1,0:T(8,128)(2,1)S(1)}, u32[]{:S(2)}, u32[]{:S(2)}) %collective-permute-start.16) | collective-permute-done | bytes 262176 | tf_op jit(solution)/shard_map/ppermute | solution.py:34
  100.1 3.6 %collective-permute-done.3.zor = bf16[128,1024]{1,0:T(8,128)(2,1)S(1)} collective-permute-done((bf16[128,1024]{1,0:T(8,128)(2,1)S(1)}, bf16[128,1024]{1,0:T(8,128)(2,1)S(1)}, u32[]{:S(2)}, u32[]{:S(2)}) %collective-permute-start.3) | collective-permute-done | bytes 262176 | tf_op jit(solution)/shard_map/ppermute | solution.py:295
  107.1 13.8 %collective-permute-done.23.prev = bf16[128,1024]{1,0:T(8,128)(2,1)S(1)} collective-permute-done((bf16[128,1024]{1,0:T(8,128)(2,1)S(1)}, bf16[128,1024]{1,0:T(8,128)(2,1)S(1)}, u32[]{:S(2)}, u32[]{:S(2)}) %collective-permute-start.23) | collective-permute-done | bytes 262176 | tf_op jit(solution)/shard_map/ppermute | solution.py:32
  122.4 16.4 %collective-permute-done.9.zl = bf16[384,1024]{1,0:T(8,128)(2,1)S(1)} collective-permute-done((bf16[384,1024]{1,0:T(8,128)(2,1)S(1)}, bf16[384,1024]{1,0:T(8,128)(2,1)S(1)}, u32[]{:S(2)}, u32[]{:S(2)}) %collective-permute-start.9) | collective-permute-done | bytes 786464 | tf_op jit(solution)/shard_map/ppermute | solution.py:299
  158.9 8.3 %shard_map.90 = (f32[1024,512]{1,0:T(8,128)S(1)}, f32[1024,128]{1,0:T(8,128)S(1)}, bf16[2048,1024]{1,0:T(8,128)(2,1)}) custom-call(s32[11]{0:T(128)S(1)} %stack.60.idx, f32[512,128]{1,0:T(8,128)S(1)} %copy-done.11, bf16[512,1024]{1,0:T(8,128)(2,1)S(1)} %pad_maximum_fusion.1.z_all, bf16[128,1024]{1,0:T(8,128)(2,1)S(1)} %copy-done.13, ...), custom_call_target="tpu_custom_call" | custom-call | flops 3221225472 | bytes 19136556 | tf_op jit(solution)/shard_map/pallas_call | solution.py:225
  167.3 2.2 copy-done.1
  169.5 5.7 %shard_map.91 = (f32[1024,512]{1,0:T(8,128)}, f32[1024,128]{1,0:T(8,128)}) custom-call(s32[11]{0:T(128)S(1)} %stack.60.idx, bf16[256,1024]{1,0:T(8,128)(2,1)} %collective-permute-done.8.za, bf16[256,1024]{1,0:T(8,128)(2,1)} %collective-permute-done.10.zb, bf16[256,1024]{1,0:T(8,128)(2,1)} %collective-permute-done.18.ya, ...), custom_call_target="tpu_custom_call" | custom-call | flops 1073741824 | bytes 9175084 | tf_op jit(solution)/shard_map/pallas_call | solution.py:225
  175.2 3.7 %all-to-all-start = ((f32[16,64,128]{2,1,0:T(8,128)}), f32[16,64,128]{2,1,0:T(8,128)S(1)}, u32[]{:S(2)}, u32[]{:S(2)}) async-start(f32[16,64,128]{2,1,0:T(8,128)} %bitcast.13), calls=%async_computation | async-start | bytes 1048576 | tf_op jit(solution)/shard_map/all_to_all | solution.py:336
  178.9 8.9 %all-to-all-done = f32[16,64,128]{2,1,0:T(8,128)S(1)} async-done(((f32[16,64,128]{2,1,0:T(8,128)}), f32[16,64,128]{2,1,0:T(8,128)S(1)}, u32[]{:S(2)}, u32[]{:S(2)}) %all-to-all-start) | async-done | bytes 524320 | tf_op jit(solution)/shard_map/all_to_all | solution.py:336
  189.5 3.8 %all-to-all-start.1 = ((f32[16,64,128]{2,1,0:T(8,128)}), f32[16,64,128]{2,1,0:T(8,128)S(1)}, u32[]{:S(2)}, u32[]{:S(2)}) async-start(f32[16,64,128]{2,1,0:T(8,128)} %broadcast_in_dim.4), calls=%async_computation.1 | async-start | bytes 1048576 | tf_op jit(solution)/shard_map/all_to_all | solution.py:339
  193.3 3.5 %shard_map.92.gram = f32[2,512,512]{2,1,0:T(8,128)S(1)} custom-call(f32[1024,512]{1,0:T(8,128)S(1)} %copy-done.18), custom_call_target="tpu_custom_call" | custom-call | flops 4294967296 | bytes 4194304 | tf_op jit(solution)/shard_map/pallas_call | solution.py:277
  198.2 4.0 %all-to-all-done.1 = f32[16,64,128]{2,1,0:T(8,128)S(1)} async-done(((f32[16,64,128]{2,1,0:T(8,128)}), f32[16,64,128]{2,1,0:T(8,128)S(1)}, u32[]{:S(2)}, u32[]{:S(2)}) %all-to-all-start.1) | async-done | bytes 524320 | tf_op jit(solution)/shard_map/all_to_all | solution.py:339
  204.1 9.2 %all-to-all-start.2 = ((f32[8,1,1]{2,1,0:T(1,128)}), f32[8,1,1]{2,1,0:T(1,128)S(1)}, u32[]{:S(2)}, u32[]{:S(2)}) async-start(f32[8,1,1]{2,1,0:T(1,128)} %broadcast_in_dim.10), calls=%async_computation.2 | async-start | bytes 8192 | tf_op jit(solution)/shard_map/all_to_all | solution.py:342
  (127 shorter events, 55.9 us)
Async XLA Ops:
  7.8 16.3 %collective-permute-start = (f32[128,1024]{1,0:T(8,128)S(1)}, f32[128,1024]{1,0:T(8,128)S(1)}, u32[]{:S(2)}, u32[]{:S(2)}) collective-permute-start(f32[128,1024]{1,0:T(8,128)S(1)} %get-tuple-element.20), channel_id=1, source_target_pairs={{0,4},{4,8},{8,12},{12,0},{1,5},{5,9},{9,13},{13,1},{2,6},{6,10},{... | collective-permute-start | bytes 1572872 | tf_op jit(solution)/shard_map/ppermute | solution.py:107
  12.5 21.9 %collective-permute-start.2 = (f32[128,1024]{1,0:T(8,128)S(1)}, f32[128,1024]{1,0:T(8,128)S(1)}, u32[]{:S(2)}, u32[]{:S(2)}) collective-permute-start(f32[128,1024]{1,0:T(8,128)S(1)} %get-tuple-element.21), channel_id=1, source_target_pairs={{0,12},{4,0},{8,4},{12,8},{1,13},{5,1},{9,5},{13,9},{2,14},{6,2},{... | collective-permute-start | bytes 1572872 | tf_op jit(solution)/shard_map/ppermute | solution.py:109
  24.2 27.3 %collective-permute-start.11 = (f32[128,1024]{1,0:T(8,128)S(1)}, f32[128,1024]{1,0:T(8,128)S(1)}, u32[]{:S(2)}, u32[]{:S(2)}) collective-permute-start(f32[128,1024]{1,0:T(8,128)S(1)} %get-tuple-element.23), channel_id=1, source_target_pairs={{0,4},{4,8},{8,12},{12,0},{1,5},{5,9},{9,13},{13,1},{2,6},{6,10},{... | collective-permute-start | bytes 1572872 | tf_op jit(solution)/shard_map/ppermute | solution.py:104
  25.0 27.8 %collective-permute-start.13 = (f32[128,1024]{1,0:T(8,128)S(1)}, f32[128,1024]{1,0:T(8,128)S(1)}, u32[]{:S(2)}, u32[]{:S(2)}) collective-permute-start(f32[128,1024]{1,0:T(8,128)S(1)} %add.146), channel_id=1, source_target_pairs={{0,12},{4,0},{8,4},{12,8},{1,13},{5,1},{9,5},{13,9},{2,14},{6,2},{... | collective-permute-start | bytes 1572872 | tf_op jit(solution)/shard_map/ppermute | solution.py:108
  37.8 38.3 %collective-permute-start.22 = (bf16[128,1024]{1,0:T(8,128)(2,1)S(1)}, bf16[128,1024]{1,0:T(8,128)(2,1)S(1)}, u32[]{:S(2)}, u32[]{:S(2)}) collective-permute-start(bf16[128,1024]{1,0:T(8,128)(2,1)S(1)} %add_convert_fusion.1), channel_id=1, source_target_pairs={{0,0},{1,32},{2,64},{3,96},{4,16},{5,48},{6,80},{7,112},{8,1},{9,3... | collective-permute-start | bytes 786440 | tf_op jit(solution)/shard_map/ppermute | solution.py:286
  48.9 16.7 %collective-permute-start.5 = (bf16[128,1024]{1,0:T(8,128)(2,1)S(1)}, bf16[128,1024]{1,0:T(8,128)(2,1)S(1)}, u32[]{:S(2)}, u32[]{:S(2)}) collective-permute-start(bf16[128,1024]{1,0:T(8,128)(2,1)S(1)} %add_convert_fusion.1), channel_id=1, source_target_pairs={{0,12},{4,0},{8,4},{12,8},{1,13},{5,1},{9,5},{13,9},{2,14},{6,2},{... | collective-permute-start | bytes 786440 | tf_op jit(solution)/shard_map/ppermute | solution.py:33
  51.5 20.9 %collective-permute-start.6 = (bf16[128,1024]{1,0:T(8,128)(2,1)S(1)}, bf16[128,1024]{1,0:T(8,128)(2,1)S(1)}, u32[]{:S(2)}, u32[]{:S(2)}) collective-permute-start(bf16[128,1024]{1,0:T(8,128)(2,1)S(1)} %add_convert_fusion.1), channel_id=1, source_target_pairs={{0,8},{4,12},{8,0},{12,4},{1,9},{5,13},{9,1},{13,5},{2,10},{6,14},... | collective-permute-start | bytes 786440 | tf_op jit(solution)/shard_map/ppermute | solution.py:34
  52.9 22.1 %collective-permute-start.26 = (bf16[128,1024]{1,0:T(8,128)(2,1)S(1)}, bf16[128,1024]{1,0:T(8,128)(2,1)S(1)}, u32[]{:S(2)}, u32[]{:S(2)}) collective-permute-start(bf16[128,1024]{1,0:T(8,128)(2,1)S(1)} %add_convert_fusion), channel_id=1, source_target_pairs={{0,0},{1,32},{2,64},{3,96},{4,16},{5,48},{6,80},{7,112},{8,1},{9,3... | collective-permute-start | bytes 786440 | tf_op jit(solution)/shard_map/ppermute | solution.py:286
  73.2 49.1 %collective-permute-start.7 = (bf16[384,1024]{1,0:T(8,128)(2,1)S(1)}, bf16[384,1024]{1,0:T(8,128)(2,1)S(1)}, u32[]{:S(2)}, u32[]{:S(2)}) collective-permute-start(bf16[384,1024]{1,0:T(8,128)(2,1)S(1)} %constant_dynamic-update-slice_fusion), channel_id=1, source_target_pairs={{0,1},{1,2},{2,3},{3,0},{4,5},{5,6},{6,7},{7,4},{8,9},{9,10},{10,1... | collective-permute-start | bytes 2359304 | tf_op jit(solution)/shard_map/ppermute | solution.py:298
  75.1 23.4 %collective-permute-start.16 = (bf16[128,1024]{1,0:T(8,128)(2,1)S(1)}, bf16[128,1024]{1,0:T(8,128)(2,1)S(1)}, u32[]{:S(2)}, u32[]{:S(2)}) collective-permute-start(bf16[128,1024]{1,0:T(8,128)(2,1)S(1)} %add_convert_fusion), channel_id=1, source_target_pairs={{0,2},{1,3},{2,0},{3,1},{4,6},{5,7},{6,4},{7,5},{8,10},{9,11},{10,... | collective-permute-start | bytes 786440 | tf_op jit(solution)/shard_map/ppermute | solution.py:34
  76.1 27.5 %collective-permute-start.3 = (bf16[128,1024]{1,0:T(8,128)(2,1)S(1)}, bf16[128,1024]{1,0:T(8,128)(2,1)S(1)}, u32[]{:S(2)}, u32[]{:S(2)}) collective-permute-start(bf16[128,1024]{1,0:T(8,128)(2,1)S(1)} %add_convert_fusion.1), channel_id=1, source_target_pairs={{0,1},{1,2},{2,3},{3,0},{4,5},{5,6},{6,7},{7,4},{8,9},{9,10},{10,1... | collective-permute-start | bytes 786440 | tf_op jit(solution)/shard_map/ppermute | solution.py:295
  76.5 27.9 %collective-permute-start.27 = (bf16[128,1024]{1,0:T(8,128)(2,1)S(1)}, bf16[128,1024]{1,0:T(8,128)(2,1)S(1)}, u32[]{:S(2)}, u32[]{:S(2)}) collective-permute-start(bf16[128,1024]{1,0:T(8,128)(2,1)S(1)} %collective-permute-done.26.own), channel_id=1, source_target_pairs={{0,32},{16,48},{32,64},{48,80},{64,96},{80,112},{96,0},{112,16},{1... | collective-permute-start | bytes 786440 | tf_op jit(solution)/shard_map/ppermute | solution.py:32
  78.6 27.8 %collective-permute-start.28 = (bf16[128,1024]{1,0:T(8,128)(2,1)S(1)}, bf16[128,1024]{1,0:T(8,128)(2,1)S(1)}, u32[]{:S(2)}, u32[]{:S(2)}) collective-permute-start(bf16[128,1024]{1,0:T(8,128)(2,1)S(1)} %collective-permute-done.26.own), channel_id=1, source_target_pairs={{0,96},{16,112},{32,0},{48,16},{64,32},{80,48},{96,64},{112,80},{1... | collective-permute-start | bytes 786440 | tf_op jit(solution)/shard_map/ppermute | solution.py:33
  103.7 17.2 %collective-permute-start.23 = (bf16[128,1024]{1,0:T(8,128)(2,1)S(1)}, bf16[128,1024]{1,0:T(8,128)(2,1)S(1)}, u32[]{:S(2)}, u32[]{:S(2)}) collective-permute-start(bf16[128,1024]{1,0:T(8,128)(2,1)S(1)} %collective-permute-done.22.own), channel_id=1, source_target_pairs={{0,32},{16,48},{32,64},{48,80},{64,96},{80,112},{96,0},{112,16},{1... | collective-permute-start | bytes 786440 | tf_op jit(solution)/shard_map/ppermute | solution.py:32
  104.4 16.5 %collective-permute-start.24 = (bf16[128,1024]{1,0:T(8,128)(2,1)S(1)}, bf16[128,1024]{1,0:T(8,128)(2,1)S(1)}, u32[]{:S(2)}, u32[]{:S(2)}) collective-permute-start(bf16[128,1024]{1,0:T(8,128)(2,1)S(1)} %collective-permute-done.22.own), channel_id=1, source_target_pairs={{0,96},{16,112},{32,0},{48,16},{64,32},{80,48},{96,64},{112,80},{1... | collective-permute-start | bytes 786440 | tf_op jit(solution)/shard_map/ppermute | solution.py:33
  106.4 36.4 %collective-permute-start.17 = (bf16[512,1024]{1,0:T(8,128)(2,1)S(1)}, bf16[512,1024]{1,0:T(8,128)(2,1)S(1)}, u32[]{:S(2)}, u32[]{:S(2)}) collective-permute-start(bf16[512,1024]{1,0:T(8,128)(2,1)S(1)} %pad_maximum_fusion.yd), channel_id=1, source_target_pairs={{0,4},{4,8},{8,12},{12,0},{1,5},{5,9},{9,13},{13,1},{2,6},{6,10},{... | collective-permute-start | bytes 3145736 | tf_op jit(solution)/shard_map/ppermute | solution.py:24
  120.8 23.5 %collective-permute-start.19 = (bf16[512,1024]{1,0:T(8,128)(2,1)S(1)}, bf16[512,1024]{1,0:T(8,128)(2,1)S(1)}, u32[]{:S(2)}, u32[]{:S(2)}) collective-permute-start(bf16[512,1024]{1,0:T(8,128)(2,1)S(1)} %pad_maximum_fusion.yd), channel_id=1, source_target_pairs={{0,12},{4,0},{8,4},{12,8},{1,13},{5,1},{9,5},{13,9},{2,14},{6,2},{... | collective-permute-start | bytes 3145736 | tf_op jit(solution)/shard_map/ppermute | solution.py:25
  120.8 17.9 %collective-permute-start.9 = (bf16[384,1024]{1,0:T(8,128)(2,1)S(1)}, bf16[384,1024]{1,0:T(8,128)(2,1)S(1)}, u32[]{:S(2)}, u32[]{:S(2)}) collective-permute-start(bf16[384,1024]{1,0:T(8,128)(2,1)S(1)} %constant_dynamic-update-slice_fusion), channel_id=1, source_target_pairs={{0,3},{1,0},{2,1},{3,2},{4,7},{5,4},{6,5},{7,6},{8,11},{9,8},{10,9... | collective-permute-start | bytes 2359304 | tf_op jit(solution)/shard_map/ppermute | solution.py:299
  120.9 28.2 %collective-permute-start.31 = (bf16[4,128,1024]{2,1,0:T(8,128)(2,1)S(1)}, bf16[4,128,1024]{2,1,0:T(8,128)(2,1)S(1)}, u32[]{:S(2)}, u32[]{:S(2)}) collective-permute-start(bf16[4,128,1024]{2,1,0:T(8,128)(2,1)S(1)} %shard_map.89.bb), channel_id=1, source_target_pairs={{0,16},{16,0},{32,48},{48,32},{64,80},{80,64},{96,112},{112,96},{1... | collective-permute-start | bytes 3145736 | tf_op jit(solution)/shard_map/ppermute | solution.py:290
  122.3 30.8 %collective-permute-start.30 = (bf16[4,128,1024]{2,1,0:T(8,128)(2,1)S(1)}, bf16[4,128,1024]{2,1,0:T(8,128)(2,1)}, u32[]{:S(2)}, u32[]{:S(2)}) collective-permute-start(bf16[4,128,1024]{2,1,0:T(8,128)(2,1)S(1)} %shard_map.88.bt), channel_id=1, source_target_pairs={{0,16},{16,0},{32,48},{48,32},{64,80},{80,64},{96,112},{112,96},{1... | collective-permute-start | bytes 3145736 | tf_op jit(solution)/shard_map/ppermute | solution.py:290
  142.8 24.4 %collective-permute-start.8 = (bf16[256,1024]{1,0:T(8,128)(2,1)}, bf16[256,1024]{1,0:T(8,128)(2,1)}, u32[]{:S(2)}, u32[]{:S(2)}) collective-permute-start(bf16[256,1024]{1,0:T(8,128)(2,1)} %pad_maximum_fusion.2), channel_id=1, source_target_pairs={{0,1},{1,2},{2,3},{3,0},{4,5},{5,6},{6,7},{7,4},{8,9},{9,10},{10,1... | collective-permute-start | bytes 1572872 | tf_op jit(solution)/shard_map/ppermute | solution.py:300
  144.4 22.9 %collective-permute-start.10 = (bf16[256,1024]{1,0:T(8,128)(2,1)}, bf16[256,1024]{1,0:T(8,128)(2,1)}, u32[]{:S(2)}, u32[]{:S(2)}) collective-permute-start(bf16[256,1024]{1,0:T(8,128)(2,1)} %slice.17), channel_id=1, source_target_pairs={{0,3},{1,0},{2,1},{3,2},{4,7},{5,4},{6,5},{7,6},{8,11},{9,8},{10,9... | collective-permute-start | bytes 1572872 | tf_op jit(solution)/shard_map/ppermute | solution.py:301
  147.9 19.3 %collective-permute-start.18 = (bf16[256,1024]{1,0:T(8,128)(2,1)}, bf16[256,1024]{1,0:T(8,128)(2,1)}, u32[]{:S(2)}, u32[]{:S(2)}) collective-permute-start(bf16[256,1024]{1,0:T(8,128)(2,1)} %slice.18), channel_id=1, source_target_pairs={{0,4},{4,8},{8,12},{12,0},{1,5},{5,9},{9,13},{13,1},{2,6},{6,10},{... | collective-permute-start | bytes 1572872 | tf_op jit(solution)/shard_map/ppermute | solution.py:26
  150.1 17.2 %collective-permute-start.20 = (bf16[256,1024]{1,0:T(8,128)(2,1)}, bf16[256,1024]{1,0:T(8,128)(2,1)}, u32[]{:S(2)}, u32[]{:S(2)}) collective-permute-start(bf16[256,1024]{1,0:T(8,128)(2,1)} %slice.19), channel_id=1, source_target_pairs={{0,12},{4,0},{8,4},{12,8},{1,13},{5,1},{9,5},{13,9},{2,14},{6,2},{... | collective-permute-start | bytes 1572872 | tf_op jit(solution)/shard_map/ppermute | solution.py:27
  (36 other events, 383.4 us)
where the time goes:
time: 221 us; the launch traced here: 220 us
  waiting for transfers between devices  93.7 us (42%)
  starting transfers between devices  71.7 us (32%)
  Pallas kernels  24.9 us (11%)
  local copies, waits for them, and re-layouts  22.2 us (10%)
  other arithmetic  4.78 us (2%)
  between operations  2.87 us (1%)
    ppermute x4, waiting for transfers between devices, gather_direct(): far = lax.ppermute(block, axis, ring(size, 2 * step))  26 us
    ppermute x2, starting transfers between devices, body(): line = lax.ppermute(half, ALL, turned())  19.5 us
    pallas_call x5, Pallas kernels, on_core(): pl.pallas_call(kernel, out_shape=outs, in_specs=[smem] + [vmem] * (len(in...  19.2 us
    unnamed x52, local copies, waits for them, and re-layouts  17.4 us
    ppermute x1, waiting for transfers between devices, body(): zl = lax.ppermute(z_rest, 'depth', ring(4, -1))  16.4 us
    ppermute x4, waiting for transfers between devices, gather_direct(): prev = lax.ppermute(block, axis, ring(size, step))  13.9 us
    ppermute x1, waiting for transfers between devices, factor_share(): far_a = lax.ppermute(fa, 'col', ring(4, 1))  10.2 us
    all_to_all x1, starting transfers between devices, body(): lax.all_to_all(jnp.broadcast_to(squares, (8, 1, 1)), 'row', 0, 0, tiled=T...  9.15 us
  transfers between devices with their start and end apart: 35, of which 13 were waited for; matrix products, arithmetic and copies ran while one was open for 2% of the time, Pallas kernels for 7%

commit v1 on v0

--- a/solution.py
+++ b/solution.py
@@ -23,8 +23,9 @@
     half = block.shape[0] // 2
     prev = lax.ppermute(block, axis, ring(size, step))
     succ = lax.ppermute(block, axis, ring(size, -step))
-    far_a = lax.ppermute(prev[:half], axis, ring(size, step))
-    far_b = lax.ppermute(succ[half:], axis, ring(size, -step))
+    cut_a, cut_b = prev[:half], succ[half:]
+    far_a = lax.ppermute(cut_a, axis, ring(size, step))
+    far_b = lax.ppermute(cut_b, axis, ring(size, -step))
     return block, prev, succ, far_a, far_b
 
 
@@ -43,28 +44,16 @@
     return lax.dot_general(a, b, (((1,), (1,)), ((), ())), preferred_element_type=F32)
 
 
-def first_kernel(idx, panel, inverse, lower, fb, sb, rows, raw, sems):
-    copies = [
-        pltpu.make_async_copy(inverse.at[256 * i : 256 * i + 256], raw.at[256 * i : 256 * i + 256], sems.at[i])
-        for i in range(4)
-    ]
-    for i, k in enumerate((3, 2)):
-        start = pl.multiple_of(idx[k] + 128, 128)
-        copies.append(
-            pltpu.make_async_copy(panel.at[pl.ds(start, 128)], rows.at[128 * i : 128 * i + 128], sems.at[4 + i])
-        )
-    for copy in copies:
-        copy.start()
-    for i in range(4):
-        copies[i].wait()
-        block = slice(256 * i, 256 * i + 256)
+def first_kernel(idx, panel, inverse, lower, fb, sb):
+    for i in range(0, 1024, 256):
         shape = (256, 1024)
-        k_index = idx[4] + 256 * i + lax.broadcasted_iota(jnp.int32, shape, 0)
+        k_index = idx[4] + i + lax.broadcasted_iota(jnp.int32, shape, 0)
         j_index = idx[5] + lax.broadcasted_iota(jnp.int32, shape, 1)
-        lower[block, :] = jnp.where(k_index >= j_index, raw[block, :].astype(F32), 0.0).astype(BF16)
-    copies[4].wait()
-    copies[5].wait()
-    both = dot_t(rows[...], lower[...])
+        block = inverse[i : i + 256, :].astype(F32)
+        lower[i : i + 256, :] = jnp.where(k_index >= j_index, block, 0.0).astype(BF16)
+    far = panel[pl.ds(pl.multiple_of(idx[3] + 128, 128), 128), :]
+    succ = panel[pl.ds(pl.multiple_of(idx[2] + 128, 128), 128), :]
+    both = dot_t(jnp.concatenate([far, succ], axis=0), lower[...])
     fb[...] = both[:128]
     sb[...] = both[128:]
 
@@ -89,18 +78,7 @@
 def factor_share(panel, inverse_factor, idx):
     piece = jax.ShapeDtypeStruct((128, 1024), F32)
     square = jax.ShapeDtypeStruct((1024, 1024), BF16)
-    lower, fb, sb = on_core(
-        first_kernel,
-        (square, piece, piece),
-        (idx, panel, inverse_factor),
-        2**29,
-        scratch=(
-            pltpu.VMEM((256, 1024), BF16),
-            pltpu.VMEM((1024, 1024), BF16),
-            pltpu.SemaphoreType.DMA((6,)),
-        ),
-        whole=2,
-    )
+    lower, fb, sb = on_core(first_kernel, (square, piece, piece), (idx, panel, inverse_factor), 2**29)
     s_b = lax.ppermute(sb, "col", ring(4, 1))
     far_b = lax.ppermute(fb, "col", ring(4, -1))
     fa, pb, pa, sa = on_core(second_kernel, (piece,) * 4, (idx, panel, lower), 2**30)
@@ -142,43 +120,68 @@
     return first[:, :R] + ((first[:, R:] + second[:, :R]) + (second[:, R:] + third))
 
 
+def columns_in(idx, sources, held, sems):
+    return [
+        [
+            pltpu.make_async_copy(src.at[idx[4 + t]], held.at[t, 128 * i : 128 * i + 128], sems.at[4 * t + i])
+            for i, src in enumerate(sources)
+        ]
+        for t in range(4)
+    ]
+
+
+def started(copies):
+    for copy in copies:
+        copy.start()
+
+
+def waited(copies):
+    for copy in copies:
+        copy.wait()
+
+
 def early_kernel(
-    idx, guess, z_all, zor, zol, zr, zl, yd, yr, yl, bt, bb, ct, cb, trailing,
-    acc, applied, b_all, z_in, y_in, b_in, mine, sems,
+    idx, guess, z0, z1, z2, z3, zor, zol, zr, zl, yd, yr, yl, bt, bb, ct, cb, trailing,
+    acc, applied, z_in, y_in, b_in, mine, b_sems, z_sems, y_sems, sem,
 ):
-    b_copies = [pltpu.make_async_copy(b, b_in.at[i], sems.at[i]) for i, b in enumerate((bt, bb, ct, cb))]
-    y_copies = [pltpu.make_async_copy(y, y_in.at[i], sems.at[4 + i]) for i, y in enumerate((yd, yr, yl))]
+    b_copies = columns_in(idx, (bt, bb, ct, cb), b_in, b_sems)
+    place = lambda t, start, src, k: pltpu.make_async_copy(
+        src, z_in.at[t, start : start + src.shape[0]], z_sems.at[k]
+    )
     z_copies = [
-        [pltpu.make_async_copy(z_all, z_in.at[0], sems.at[7])],
+        [place(0, 128 * i, src, i) for i, src in enumerate((z0, z1, z2, z3))],
+        [place(1, 0, zor, 4), place(1, 128, zr, 5)],
+        [place(2, 0, zol, 6), place(2, 128, zl, 7)],
+    ]
+    y_copies = [
         [
-            pltpu.make_async_copy(zor, z_in.at[1, :128], sems.at[8]),
-            pltpu.make_async_copy(zr, z_in.at[1, 128:], sems.at[9]),
-        ],
-        [
-            pltpu.make_async_copy(zol, z_in.at[2, :128], sems.at[10]),
-            pltpu.make_async_copy(zl, z_in.at[2, 128:], sems.at[11]),
-        ],
+            pltpu.make_async_copy(
+                src.at[128 * t : 128 * t + 128], y_in.at[t, 128 * i : 128 * i + 128], y_sems.at[3 * t + i]
+            )
+            for i, src in enumerate((yd, yr, yl))
+        ]
+        for t in range(4)
     ]
     columns = pl.ds(pl.multiple_of(idx[10] * 512, 512), 512)
-    last = pltpu.make_async_copy(trailing.at[:, columns], mine, sems.at[12])
-    for copy in b_copies + z_copies[0] + y_copies + z_copies[1] + z_copies[2] + [last]:
-        copy.start()
-    for copy in b_copies:
-        copy.wait()
+    last = pltpu.make_async_copy(trailing.at[:, columns], mine, sem)
+    z_copies.append([last])
+
+    def stage(t):
+        started(b_copies[t] + z_copies[t] + y_copies[t])
+
+    stage(0)
+    stage(1)
     z_total = y_total = None
     for t in range(4):
-        b = jnp.concatenate([b_in[i, idx[4 + t]] for i in range(4)], axis=0)
-        b_all[512 * t : 512 * t + 512, :] = b
+        waited(b_copies[t])
+        if 1 <= t < 3:
+            stage(t + 1)
         if t < 3:
-            for copy in z_copies[t]:
-                copy.wait()
-            part = dot_t(z_in[t], b)
+            waited(z_copies[t])
+            part = dot_t(z_in[t], b_in[t])
             z_total = part if t == 0 else z_total + part
-        if t == 0:
-            for copy in y_copies:
-                copy.wait()
-        y = jnp.concatenate([y_in[i, 128 * t : 128 * t + 128, :] for i in range(3)], axis=0)
-        part = dot_t(y, b)
+        waited(y_copies[t])
+        part = dot_t(y_in[t], b_in[t])
         y_total = part if t == 0 else y_total + part
     last.wait()
     for h in range(2):
@@ -195,12 +198,31 @@
     applied[...] = full_dot(acc[...], guess[...])
 
 
-def late_kernel(idx, za, zb, ya, yb, b_all, acc, early, guess, updated, applied, part):
-    z = jnp.concatenate([za[...], zb[...], yb[128:, :]], axis=0)
-    z = dot_t(z, b_all[1536:, :])
+def late_kernel(
+    idx, guess, acc, early, zo, za, zb, ya, yb, bt, bb, ct, cb,
+    updated, applied, z_in, y_in, b_in, part, b_sems, sems,
+):
+    b_copies = columns_in(idx, (bt, bb, ct, cb), b_in, b_sems)
+    z_copies = [
+        pltpu.make_async_copy(zo, z_in.at[:128], sems.at[0]),
+        pltpu.make_async_copy(za, z_in.at[128:320], sems.at[1]),
+        pltpu.make_async_copy(zb, z_in.at[320:512], sems.at[5]),
+        pltpu.make_async_copy(yb.at[128:], z_in.at[512:], sems.at[2]),
+    ]
+    y_copies = [
+        pltpu.make_async_copy(ya, y_in.at[:256], sems.at[3]),
+        pltpu.make_async_copy(yb.at[:128], y_in.at[256:], sems.at[4]),
+    ]
+    started(b_copies[3] + z_copies + y_copies)
+    for t in range(3):
+        started(b_copies[t])
+    waited(b_copies[3] + z_copies)
+    z = dot_t(z_in[...], b_in[3])
+    waited(y_copies)
     y = z[512:]
-    for t, block in enumerate((ya[:128, :], ya[128:, :], yb[:128, :])):
-        y = y + dot_t(block, b_all[512 * t : 512 * t + 512, :])
+    for t in range(3):
+        waited(b_copies[t])
+        y = y + dot_t(y_in[128 * t : 128 * t + 128, :], b_in[t])
     for h in range(2):
         cols = pl.ds(pl.multiple_of(idx[8 + h] * 256, 256), 256)
         half = slice(256 * h, 256 * h + 256)
@@ -259,10 +281,12 @@
         )
 
 
-def correct_kernel(gram, residual, correction):
+def correct_kernel(gram, residual, correction, squares):
     for i in range(2):
         rows = slice(BS * i, BS * i + BS)
         correction[rows, :] = full_dot(gram[i], residual[rows, :])
+    total = (residual[...] * residual[...]).reshape(128, 8, R).sum(axis=0)
+    squares[...] = jnp.broadcast_to(total[None], (8, 8, R))
 
 
 def body(trailing, panel, inverse_factor, block_inverse, guess, target):
@@ -290,15 +314,10 @@
         b_other.append(lax.ppermute(packed, "row", [(i, i ^ 1) for i in range(8)]))
 
     z_parts = gather_direct(top, "col", 1, 4)
-    z_all = joined(z_parts)
     y_all = joined(gather_direct(bottom, "depth", 1, 4))
-    z_own_r = lax.ppermute(top, "depth", ring(4, 1))
-    z_own_l = lax.ppermute(top, "depth", ring(4, -1))
+    _, z_own_r, z_own_l, z_own_far = gather_direct(top, "depth", 1, 4)
     z_rest = joined(z_parts[1:])
-    zr = lax.ppermute(z_rest, "depth", ring(4, 1))
-    zl = lax.ppermute(z_rest, "depth", ring(4, -1))
-    za = lax.ppermute(joined([z_own_r, zr[:128]]), "depth", ring(4, 1))
-    zb = lax.ppermute(zl[128:], "depth", ring(4, -1))
+    _, zr, zl, za, zb = gather_ring(z_rest, "depth", 1, 4)
     yd, yr, yl, ya, yb = gather_ring(y_all, "col", 1, 4)
 
     offsets = [256 * ((col_id + k) % 4) for k in (0, 3, 1, 2)]
@@ -310,27 +329,39 @@
 
     tile = jax.ShapeDtypeStruct((1024, 512), F32)
     narrow = jax.ShapeDtypeStruct((1024, R), F32)
-    acc, early, b_all = on_core(
+    acc, early = on_core(
         early_kernel,
-        (tile, narrow, jax.ShapeDtypeStruct((2048, 1024), BF16)),
-        (idx, guess, z_all, z_own_r, z_own_l, zr, zl, yd, yr, yl, *b_own, *b_other, trailing),
+        (tile, narrow),
+        (idx, guess, *z_parts, z_own_r, z_own_l, zr, zl, yd, yr, yl, *b_own, *b_other, trailing),
         2 * 512 * 1024 * (896 * 3 + 384),
-        vmem_mib=40,
+        vmem_mib=60,
         scratch=(
             pltpu.VMEM((3, 512, 1024), BF16),
-            pltpu.VMEM((3, 512, 1024), BF16),
-            pltpu.VMEM((4, 4, 128, 1024), BF16),
+            pltpu.VMEM((4, 384, 1024), BF16),
+            pltpu.VMEM((4, 512, 1024), BF16),
             pltpu.VMEM((1024, 512), F32),
-            pltpu.SemaphoreType.DMA((13,)),
+            pltpu.SemaphoreType.DMA((16,)),
+            pltpu.SemaphoreType.DMA((8,)),
+            pltpu.SemaphoreType.DMA((12,)),
+            pltpu.SemaphoreType.DMA,
         ),
-        whole=13,
+        whole=16,
     )
     updated, applied = on_core(
         late_kernel,
         (tile, narrow),
-        (idx, za, zb, ya, yb, b_all, acc, early, guess),
+        (idx, guess, acc, early, z_own_far, za, zb, ya, yb, *b_own, *b_other),
         2 * 512 * 1024 * 1024,
-        scratch=(pltpu.VMEM((640, 512), F32),),
+        vmem_mib=60,
+        scratch=(
+            pltpu.VMEM((640, 1024), BF16),
+            pltpu.VMEM((384, 1024), BF16),
+            pltpu.VMEM((4, 512, 1024), BF16),
+            pltpu.VMEM((640, 512), F32),
+            pltpu.SemaphoreType.DMA((16,)),
+            pltpu.SemaphoreType.DMA((6,)),
+        ),
+        whole=9,
     )
 
     pieces = lax.all_to_all(applied.reshape(16, 64, R), PLANE, 0, 0, tiled=True)
@@ -338,15 +369,14 @@
     part = lax.dynamic_slice_in_dim(target, piece_id * 64, 64, 0) - pieces.sum(axis=0)
     residual = lax.all_to_all(jnp.broadcast_to(part[None], (16, 64, R)), PLANE, 0, 0, tiled=True)
     residual = residual.reshape(1024, R)
-    squares = jnp.sum(residual * residual)
-    squares = lax.all_to_all(jnp.broadcast_to(squares, (8, 1, 1)), "row", 0, 0, tiled=True).sum(axis=0)
-    residual_rms = jnp.sqrt(squares / (N * R))
-    correction = pl.pallas_call(
+    correction, squares = pl.pallas_call(
         correct_kernel,
-        out_shape=jax.ShapeDtypeStruct((1024, R), F32),
+        out_shape=(jax.ShapeDtypeStruct((1024, R), F32), jax.ShapeDtypeStruct((8, 8, R), F32)),
         cost_estimate=pl.CostEstimate(flops=2**30, bytes_accessed=2**22, transcendentals=0),
         compiler_params=pltpu.CompilerParams(vmem_limit_bytes=16 * 1024 * 1024),
     )(gram, residual)
+    squares = lax.all_to_all(squares, "row", 0, 0, tiled=True).sum()
+    residual_rms = jnp.sqrt(squares / (N * R))
     return (updated, correction, residual_rms.reshape(1))
 
 

time: 221 us -> 241 us (1.090)
  starting transfers between devices: 71.7 us -> 93.6 us
  blocking collectives: 0 us -> 13.4 us
  local copies, waits for them, and re-layouts: 22.2 us -> 11.6 us
  waiting for transfers between devices: 93.7 us -> 87 us
  Pallas kernels: 24.9 us -> 29.9 us
  other arithmetic: 4.78 us -> 1.82 us
    ppermute x8 -> x4, waiting for transfers between devices: 20 us -> 0.01 us  [the longest x2 0.01 us: gather_ring(): far_a = lax.ppermute(cut_a, axis, ring(size, step))]
    ppermute x4 -> x5, waiting for transfers between devices: 13.9 us -> 31.3 us  [gather_direct(): prev = lax.ppermute(block, axis, ring(size, step))]
    ppermute x8 -> x4, starting transfers between devices: 8.43 us -> 25.8 us  [the longest x2 19.9 us: gather_ring(): far_a = lax.ppermute(cut_a, axis, ring(size, step))]
    ppermute x4 -> x5, waiting for transfers between devices: 26 us -> 9.18 us  [gather_direct(): far = lax.ppermute(block, axis, ring(size, 2 * step))]
    all_to_all x0 -> x1, blocking collectives: none -> 13.4 us  [body(): squares = lax.all_to_all(squares, 'row', 0, 0, tiled=True).sum()]
    unnamed x52 -> x44, local copies, waits for them, and re-layouts: 17.4 us -> 7.22 us
    ppermute x1, waiting for transfers between devices: 10.2 us -> 0.12 us  [factor_share(): far_a = lax.ppermute(fa, 'col', ring(4, 1))]
    ppermute x1 -> x2, waiting for transfers between devices: 0.01 us -> 9.99 us  [gather_ring(): prev = lax.ppermute(block, axis, ring(size, step))]
  transfers between devices with their start and end apart: 35 -> 35, of which waited for: 13 -> 16; matrix products, arithmetic and copies ran while one was open for 2% -> 2% of each run, Pallas kernels for 7% -> 7%
where the time goes in v1:
time: 241 us; the launch traced here: 240 us
  starting transfers between devices  93.6 us (39%)
  waiting for transfers between devices  87 us (36%)
  Pallas kernels  29.9 us (12%)
  blocking collectives  13.4 us (6%)
  local copies, waits for them, and re-layouts  11.6 us (5%)
  between operations  2.91 us (1%)
    ppermute x5, waiting for transfers between devices, gather_direct(): prev = lax.ppermute(block, axis, ring(size, step))  31.3 us
    pallas_call x5, Pallas kernels, on_core(): pl.pallas_call(kernel, out_shape=outs, in_specs=[smem] + [vmem] * (len(in...  24.2 us
    ppermute x2, starting transfers between devices, gather_ring(): far_a = lax.ppermute(cut_a, axis, ring(size, step))  19.9 us
    ppermute x2, starting transfers between devices, body(): line = lax.ppermute(half, ALL, turned())  15.7 us
    all_to_all x1, blocking collectives, body(): squares = lax.all_to_all(squares, 'row', 0, 0, tiled=True).sum()  13.4 us
    ppermute x5, starting transfers between devices, gather_direct(): succ = lax.ppermute(block, axis, ring(size, -step))  10.9 us
    ppermute x2, waiting for transfers between devices, gather_ring(): prev = lax.ppermute(block, axis, ring(size, step))  9.99 us
    ppermute x1, waiting for transfers between devices, factor_share(): s_b = lax.ppermute(sb, 'col', ring(4, 1))  9.82 us
  transfers between devices with their start and end apart: 35, of which 16 were waited for; matrix products, arithmetic and copies ran while one was open for 2% of the time, Pallas kernels for 7%

profile of v1, /device:TPU:1, one launch (start us, length us, event | category | flops | bytes accessed | tf_op | source)
XLA Modules:
  0.0 240.2 jit_solution(10873338233578256800)
XLA Ops:
  5.3 4.6 %collective-permute-start.11 = (f32[128,1024]{1,0:T(8,128)S(1)}, f32[128,1024]{1,0:T(8,128)S(1)}, u32[]{:S(2)}, u32[]{:S(2)}) collective-permute-start(f32[128,1024]{1,0:T(8,128)S(1)} %get-tuple-element.26), channel_id=1, source_target_pairs={{0,12},{4,0},{8,4},{12,8},{1,13},{5,1},{9,5},{13,9},{2,14},{6,2},{... | collective-permute-start | bytes 1572872 | tf_op jit(solution)/shard_map/ppermute | solution.py:83
  12.0 8.6 %collective-permute-done.11 = f32[128,1024]{1,0:T(8,128)S(1)} collective-permute-done((f32[128,1024]{1,0:T(8,128)S(1)}, f32[128,1024]{1,0:T(8,128)S(1)}, u32[]{:S(2)}, u32[]{:S(2)}) %collective-permute-start.11) | collective-permute-done | bytes 524320 | tf_op jit(solution)/shard_map/ppermute | solution.py:83
  20.6 3.5 %collective-permute-start.12 = (f32[128,1024]{1,0:T(8,128)S(1)}, f32[128,1024]{1,0:T(8,128)S(1)}, u32[]{:S(2)}, u32[]{:S(2)}) collective-permute-start(f32[128,1024]{1,0:T(8,128)S(1)} %add.146), channel_id=1, source_target_pairs={{0,12},{4,0},{8,4},{12,8},{1,13},{5,1},{9,5},{13,9},{2,14},{6,2},{... | collective-permute-start | bytes 1572872 | tf_op jit(solution)/shard_map/ppermute | solution.py:86
  27.0 9.8 %collective-permute-done.10 = f32[128,1024]{1,0:T(8,128)S(1)} collective-permute-done((f32[128,1024]{1,0:T(8,128)S(1)}, f32[128,1024]{1,0:T(8,128)S(1)}, u32[]{:S(2)}, u32[]{:S(2)}) %collective-permute-start.10) | collective-permute-done | bytes 524320 | tf_op jit(solution)/shard_map/ppermute | solution.py:82
  43.8 12.1 %collective-permute-start.22 = (bf16[128,1024]{1,0:T(8,128)(2,1)S(1)}, bf16[128,1024]{1,0:T(8,128)(2,1)S(1)}, u32[]{:S(2)}, u32[]{:S(2)}) collective-permute-start(bf16[128,1024]{1,0:T(8,128)(2,1)S(1)} %add_convert_fusion), channel_id=1, source_target_pairs={{0,0},{1,32},{2,64},{3,96},{4,16},{5,48},{6,80},{7,112},{8,1},{9,3... | collective-permute-start | bytes 786440 | tf_op jit(solution)/shard_map/ppermute | solution.py:310
  56.3 3.5 %collective-permute-start.18 = (bf16[128,1024]{1,0:T(8,128)(2,1)S(1)}, bf16[128,1024]{1,0:T(8,128)(2,1)S(1)}, u32[]{:S(2)}, u32[]{:S(2)}) collective-permute-start(bf16[128,1024]{1,0:T(8,128)(2,1)S(1)} %add_convert_fusion.1.z0), channel_id=1, source_target_pairs={{0,0},{1,32},{2,64},{3,96},{4,16},{5,48},{6,80},{7,112},{8,1},{9,3... | collective-permute-start | bytes 786440 | tf_op jit(solution)/shard_map/ppermute | solution.py:310
  64.8 6.9 %collective-permute-start.24 = (bf16[128,1024]{1,0:T(8,128)(2,1)S(1)}, bf16[128,1024]{1,0:T(8,128)(2,1)S(1)}, u32[]{:S(2)}, u32[]{:S(2)}) collective-permute-start(bf16[128,1024]{1,0:T(8,128)(2,1)S(1)} %collective-permute-done.22.own), channel_id=1, source_target_pairs={{0,96},{16,112},{32,0},{48,16},{64,32},{80,48},{96,64},{112,80},{1... | collective-permute-start | bytes 786440 | tf_op jit(solution)/shard_map/ppermute | solution.py:34
  71.7 22.1 %collective-permute-done.3.z1 = bf16[128,1024]{1,0:T(8,128)(2,1)S(1)} collective-permute-done((bf16[128,1024]{1,0:T(8,128)(2,1)S(1)}, bf16[128,1024]{1,0:T(8,128)(2,1)S(1)}, u32[]{:S(2)}, u32[]{:S(2)}) %collective-permute-start.3) | collective-permute-done | bytes 262176 | tf_op jit(solution)/shard_map/ppermute | solution.py:33
  93.8 3.2 %collective-permute-start.19 = (bf16[128,1024]{1,0:T(8,128)(2,1)S(1)}, bf16[128,1024]{1,0:T(8,128)(2,1)S(1)}, u32[]{:S(2)}, u32[]{:S(2)}) collective-permute-start(bf16[128,1024]{1,0:T(8,128)(2,1)S(1)} %collective-permute-done.18.own), channel_id=1, source_target_pairs={{0,32},{16,48},{32,64},{48,80},{64,96},{80,112},{96,0},{112,16},{1... | collective-permute-start | bytes 786440 | tf_op jit(solution)/shard_map/ppermute | solution.py:33
  98.9 4.0 %collective-permute-done.25.far = bf16[128,1024]{1,0:T(8,128)(2,1)S(1)} collective-permute-done((bf16[128,1024]{1,0:T(8,128)(2,1)S(1)}, bf16[128,1024]{1,0:T(8,128)(2,1)S(1)}, u32[]{:S(2)}, u32[]{:S(2)}) %collective-permute-start.25) | collective-permute-done | bytes 262176 | tf_op jit(solution)/shard_map/ppermute | solution.py:35
  102.9 6.1 %collective-permute-done.19.prev = bf16[128,1024]{1,0:T(8,128)(2,1)S(1)} collective-permute-done((bf16[128,1024]{1,0:T(8,128)(2,1)S(1)}, bf16[128,1024]{1,0:T(8,128)(2,1)S(1)}, u32[]{:S(2)}, u32[]{:S(2)}) %collective-permute-start.19) | collective-permute-done | bytes 262176 | tf_op jit(solution)/shard_map/ppermute | solution.py:33
  109.0 3.3 %collective-permute-start.5 = (bf16[128,1024]{1,0:T(8,128)(2,1)S(1)}, bf16[128,1024]{1,0:T(8,128)(2,1)S(1)}, u32[]{:S(2)}, u32[]{:S(2)}) collective-permute-start(bf16[128,1024]{1,0:T(8,128)(2,1)S(1)} %add_convert_fusion.1.z0), channel_id=1, source_target_pairs={{0,8},{4,12},{8,0},{12,4},{1,9},{5,13},{9,1},{13,5},{2,10},{6,14},... | collective-permute-start | bytes 786440 | tf_op jit(solution)/shard_map/ppermute | solution.py:35
  123.0 3.6 %collective-permute-done.17.yl = bf16[512,1024]{1,0:T(8,128)(2,1)S(1)} collective-permute-done((bf16[512,1024]{1,0:T(8,128)(2,1)S(1)}, bf16[512,1024]{1,0:T(8,128)(2,1)S(1)}, u32[]{:S(2)}, u32[]{:S(2)}) %collective-permute-start.17) | collective-permute-done | bytes 1048608 | tf_op jit(solution)/shard_map/ppermute | solution.py:25
  128.5 10.0 %collective-permute-done.8.zr = bf16[384,1024]{1,0:T(8,128)(2,1)S(1)} collective-permute-done((bf16[384,1024]{1,0:T(8,128)(2,1)S(1)}, bf16[384,1024]{1,0:T(8,128)(2,1)S(1)}, u32[]{:S(2)}, u32[]{:S(2)}) %collective-permute-start.8) | collective-permute-done | bytes 786464 | tf_op jit(solution)/shard_map/ppermute | solution.py:24
  138.5 18.7 %collective-permute-start.31 = (bf16[256,1024]{1,0:T(8,128)(2,1)}, bf16[256,1024]{1,0:T(8,128)(2,1)}, u32[]{:S(2)}, u32[]{:S(2)}) collective-permute-start(bf16[256,1024]{1,0:T(8,128)(2,1)} %slice.18), channel_id=1, source_target_pairs={{0,4},{4,8},{8,12},{12,0},{1,5},{5,9},{9,13},{13,1},{2,6},{6,10},{... | collective-permute-start | bytes 1572872 | tf_op jit(solution)/shard_map/ppermute | solution.py:27
  157.2 4.3 %collective-permute-start.32 = (bf16[256,1024]{1,0:T(8,128)(2,1)}, bf16[256,1024]{1,0:T(8,128)(2,1)}, u32[]{:S(2)}, u32[]{:S(2)}) collective-permute-start(bf16[256,1024]{1,0:T(8,128)(2,1)} %slice.19), channel_id=1, source_target_pairs={{0,12},{4,0},{8,4},{12,8},{1,13},{5,1},{9,5},{13,9},{2,14},{6,2},{... | collective-permute-start | bytes 1572872 | tf_op jit(solution)/shard_map/ppermute | solution.py:28
  166.7 10.9 %shard_map.90 = (f32[1024,512]{1,0:T(8,128)}, f32[1024,128]{1,0:T(8,128)}) custom-call(s32[11]{0:T(128)} %stack.60.idx, f32[512,128]{1,0:T(8,128)} %guess.3, bf16[128,1024]{1,0:T(8,128)(2,1)} %copy-done.13, bf16[128,1024]{1,0:T(8,128)(2,1)} %copy-done.14, bf16[128,1024]{1,0:T(8,128)(2,1)} %copy-done.15, bf16[128,1024]{1,0:T(8,128)(2,1)} %copy-done.16, ...), custom_call_target="tpu_custom_call" | custom-call | flops 3221225472 | bytes 19136556 | tf_op jit(solution)/shard_map/pallas_call | solution.py:247
  179.7 8.8 %shard_map.91 = (f32[1024,512]{1,0:T(8,128)}, f32[1024,128]{1,0:T(8,128)}) custom-call(s32[11]{0:T(128)} %stack.60.idx, f32[512,128]{1,0:T(8,128)} %guess.3, f32[1024,512]{1,0:T(8,128)} %get-tuple-element.27.acc, f32[1024,128]{1,0:T(8,128)} %get-tuple-element.28.early, bf16[128,1024]{1,0:T(8,128)(2,1)} %copy-done.20, bf16[192,1024]{1,0:T(8,128)(2,1)} %copy-done.17, ...), custom_call_target="tpu_custom_call" | custom-call | flops 1073741824 | bytes 9175084 | tf_op jit(solution)/shard_map/pallas_call | solution.py:247
  188.5 8.7 %all-to-all-start = ((f32[16,64,128]{2,1,0:T(8,128)}), f32[16,64,128]{2,1,0:T(8,128)S(1)}, u32[]{:S(2)}, u32[]{:S(2)}) async-start(f32[16,64,128]{2,1,0:T(8,128)} %bitcast.17), calls=%async_computation | async-start | bytes 1048576 | tf_op jit(solution)/shard_map/all_to_all | solution.py:367
  197.2 9.3 %all-to-all-done = f32[16,64,128]{2,1,0:T(8,128)S(1)} async-done(((f32[16,64,128]{2,1,0:T(8,128)}), f32[16,64,128]{2,1,0:T(8,128)S(1)}, u32[]{:S(2)}, u32[]{:S(2)}) %all-to-all-start) | async-done | bytes 524320 | tf_op jit(solution)/shard_map/all_to_all | solution.py:367
  208.2 3.8 %all-to-all-start.1 = ((f32[16,64,128]{2,1,0:T(8,128)}), f32[16,64,128]{2,1,0:T(8,128)S(1)}, u32[]{:S(2)}, u32[]{:S(2)}) async-start(f32[16,64,128]{2,1,0:T(8,128)} %broadcast_in_dim.2), calls=%async_computation.1 | async-start | bytes 1048576 | tf_op jit(solution)/shard_map/all_to_all | solution.py:370
  212.0 3.5 %shard_map.92.gram = f32[2,512,512]{2,1,0:T(8,128)S(1)} custom-call(f32[1024,512]{1,0:T(8,128)S(1)} %copy-done.4), custom_call_target="tpu_custom_call" | custom-call | flops 4294967296 | bytes 4194304 | tf_op jit(solution)/shard_map/pallas_call | solution.py:301
  216.8 3.9 %all-to-all-done.1 = f32[16,64,128]{2,1,0:T(8,128)S(1)} async-done(((f32[16,64,128]{2,1,0:T(8,128)}), f32[16,64,128]{2,1,0:T(8,128)S(1)}, u32[]{:S(2)}, u32[]{:S(2)}) %all-to-all-start.1) | async-done | bytes 524320 | tf_op jit(solution)/shard_map/all_to_all | solution.py:370
  224.4 13.4 %all_to_all.15 = f32[8,8,128]{2,1,0:T(8,128)S(1)} all-to-all(f32[8,8,128]{2,1,0:T(8,128)S(1)} %get-tuple-element.32), channel_id=1, replica_groups=mesh['row'=8,'col'=4,'depth'=4] {'row'}, dimensions={0} | all-to-all | bytes 65536 | tf_op jit(solution)/shard_map/all_to_all | solution.py:378
  (116 shorter events, 50.6 us)
Async XLA Ops:
  11.9 25.0 %collective-permute-start.10 = (f32[128,1024]{1,0:T(8,128)S(1)}, f32[128,1024]{1,0:T(8,128)S(1)}, u32[]{:S(2)}, u32[]{:S(2)}) collective-permute-start(f32[128,1024]{1,0:T(8,128)S(1)} %get-tuple-element.24), channel_id=1, source_target_pairs={{0,4},{4,8},{8,12},{12,0},{1,5},{5,9},{9,13},{13,1},{2,6},{6,10},{... | collective-permute-start | bytes 1572872 | tf_op jit(solution)/shard_map/ppermute | solution.py:82
  20.6 16.2 %collective-permute-start.12 = (f32[128,1024]{1,0:T(8,128)S(1)}, f32[128,1024]{1,0:T(8,128)S(1)}, u32[]{:S(2)}, u32[]{:S(2)}) collective-permute-start(f32[128,1024]{1,0:T(8,128)S(1)} %add.146), channel_id=1, source_target_pairs={{0,12},{4,0},{8,4},{12,8},{1,13},{5,1},{9,5},{13,9},{2,14},{6,2},{... | collective-permute-start | bytes 1572872 | tf_op jit(solution)/shard_map/ppermute | solution.py:86
  24.1 32.0 %collective-permute-start.2 = (f32[128,1024]{1,0:T(8,128)S(1)}, f32[128,1024]{1,0:T(8,128)S(1)}, u32[]{:S(2)}, u32[]{:S(2)}) collective-permute-start(f32[128,1024]{1,0:T(8,128)S(1)} %get-tuple-element.22), channel_id=1, source_target_pairs={{0,12},{4,0},{8,4},{12,8},{1,13},{5,1},{9,5},{13,9},{2,14},{6,2},{... | collective-permute-start | bytes 1572872 | tf_op jit(solution)/shard_map/ppermute | solution.py:87
  25.7 30.5 %collective-permute-start.1 = (f32[128,1024]{1,0:T(8,128)S(1)}, f32[128,1024]{1,0:T(8,128)S(1)}, u32[]{:S(2)}, u32[]{:S(2)}) collective-permute-start(f32[128,1024]{1,0:T(8,128)S(1)} %add.142), channel_id=1, source_target_pairs={{0,4},{4,8},{8,12},{12,0},{1,5},{5,9},{9,13},{13,1},{2,6},{6,10},{... | collective-permute-start | bytes 1572872 | tf_op jit(solution)/shard_map/ppermute | solution.py:88
  38.3 17.6 %collective-permute-start.14 = (bf16[128,1024]{1,0:T(8,128)(2,1)S(1)}, bf16[128,1024]{1,0:T(8,128)(2,1)S(1)}, u32[]{:S(2)}, u32[]{:S(2)}) collective-permute-start(bf16[128,1024]{1,0:T(8,128)(2,1)S(1)} %add_convert_fusion), channel_id=1, source_target_pairs={{0,3},{1,0},{2,1},{3,2},{4,7},{5,4},{6,5},{7,6},{8,11},{9,8},{10,9... | collective-permute-start | bytes 786440 | tf_op jit(solution)/shard_map/ppermute | solution.py:34
  39.8 16.1 %collective-permute-start.15 = (bf16[128,1024]{1,0:T(8,128)(2,1)S(1)}, bf16[128,1024]{1,0:T(8,128)(2,1)S(1)}, u32[]{:S(2)}, u32[]{:S(2)}) collective-permute-start(bf16[128,1024]{1,0:T(8,128)(2,1)S(1)} %add_convert_fusion), channel_id=1, source_target_pairs={{0,2},{1,3},{2,0},{3,1},{4,6},{5,7},{6,4},{7,5},{8,10},{9,11},{10,... | collective-permute-start | bytes 786440 | tf_op jit(solution)/shard_map/ppermute | solution.py:35
  43.8 18.8 %collective-permute-start.22 = (bf16[128,1024]{1,0:T(8,128)(2,1)S(1)}, bf16[128,1024]{1,0:T(8,128)(2,1)S(1)}, u32[]{:S(2)}, u32[]{:S(2)}) collective-permute-start(bf16[128,1024]{1,0:T(8,128)(2,1)S(1)} %add_convert_fusion), channel_id=1, source_target_pairs={{0,0},{1,32},{2,64},{3,96},{4,16},{5,48},{6,80},{7,112},{8,1},{9,3... | collective-permute-start | bytes 786440 | tf_op jit(solution)/shard_map/ppermute | solution.py:310
  56.0 64.8 %collective-permute-start.16 = (bf16[512,1024]{1,0:T(8,128)(2,1)S(1)}, bf16[512,1024]{1,0:T(8,128)(2,1)S(1)}, u32[]{:S(2)}, u32[]{:S(2)}) collective-permute-start(bf16[512,1024]{1,0:T(8,128)(2,1)S(1)} %pad_maximum_fusion.yd), channel_id=1, source_target_pairs={{0,4},{4,8},{8,12},{12,0},{1,5},{5,9},{9,13},{13,1},{2,6},{6,10},{... | collective-permute-start | bytes 3145736 | tf_op jit(solution)/shard_map/ppermute | solution.py:24
  59.8 34.0 %collective-permute-start.3 = (bf16[128,1024]{1,0:T(8,128)(2,1)S(1)}, bf16[128,1024]{1,0:T(8,128)(2,1)S(1)}, u32[]{:S(2)}, u32[]{:S(2)}) collective-permute-start(bf16[128,1024]{1,0:T(8,128)(2,1)S(1)} %add_convert_fusion.1.z0), channel_id=1, source_target_pairs={{0,4},{4,8},{8,12},{12,0},{1,5},{5,9},{9,13},{13,1},{2,6},{6,10},{... | collective-permute-start | bytes 786440 | tf_op jit(solution)/shard_map/ppermute | solution.py:33
  60.2 33.6 %collective-permute-start.4 = (bf16[128,1024]{1,0:T(8,128)(2,1)S(1)}, bf16[128,1024]{1,0:T(8,128)(2,1)S(1)}, u32[]{:S(2)}, u32[]{:S(2)}) collective-permute-start(bf16[128,1024]{1,0:T(8,128)(2,1)S(1)} %add_convert_fusion.1.z0), channel_id=1, source_target_pairs={{0,12},{4,0},{8,4},{12,8},{1,13},{5,1},{9,5},{13,9},{2,14},{6,2},{... | collective-permute-start | bytes 786440 | tf_op jit(solution)/shard_map/ppermute | solution.py:34
  62.6 34.5 %collective-permute-start.23 = (bf16[128,1024]{1,0:T(8,128)(2,1)S(1)}, bf16[128,1024]{1,0:T(8,128)(2,1)S(1)}, u32[]{:S(2)}, u32[]{:S(2)}) collective-permute-start(bf16[128,1024]{1,0:T(8,128)(2,1)S(1)} %collective-permute-done.22.own), channel_id=1, source_target_pairs={{0,32},{16,48},{32,64},{48,80},{64,96},{80,112},{96,0},{112,16},{1... | collective-permute-start | bytes 786440 | tf_op jit(solution)/shard_map/ppermute | solution.py:33
  64.8 32.3 %collective-permute-start.24 = (bf16[128,1024]{1,0:T(8,128)(2,1)S(1)}, bf16[128,1024]{1,0:T(8,128)(2,1)S(1)}, u32[]{:S(2)}, u32[]{:S(2)}) collective-permute-start(bf16[128,1024]{1,0:T(8,128)(2,1)S(1)} %collective-permute-done.22.own), channel_id=1, source_target_pairs={{0,96},{16,112},{32,0},{48,16},{64,32},{80,48},{96,64},{112,80},{1... | collective-permute-start | bytes 786440 | tf_op jit(solution)/shard_map/ppermute | solution.py:34
  97.0 15.3 %collective-permute-start.20 = (bf16[128,1024]{1,0:T(8,128)(2,1)S(1)}, bf16[128,1024]{1,0:T(8,128)(2,1)S(1)}, u32[]{:S(2)}, u32[]{:S(2)}) collective-permute-start(bf16[128,1024]{1,0:T(8,128)(2,1)S(1)} %collective-permute-done.18.own), channel_id=1, source_target_pairs={{0,96},{16,112},{32,0},{48,16},{64,32},{80,48},{96,64},{112,80},{1... | collective-permute-start | bytes 786440 | tf_op jit(solution)/shard_map/ppermute | solution.py:34
  97.0 17.1 %collective-permute-start.21 = (bf16[128,1024]{1,0:T(8,128)(2,1)S(1)}, bf16[128,1024]{1,0:T(8,128)(2,1)S(1)}, u32[]{:S(2)}, u32[]{:S(2)}) collective-permute-start(bf16[128,1024]{1,0:T(8,128)(2,1)S(1)} %collective-permute-done.18.own), channel_id=1, source_target_pairs={{0,64},{16,80},{32,96},{48,112},{64,0},{80,16},{96,32},{112,48},{1... | collective-permute-start | bytes 786440 | tf_op jit(solution)/shard_map/ppermute | solution.py:35
  102.9 23.6 %collective-permute-start.17 = (bf16[512,1024]{1,0:T(8,128)(2,1)S(1)}, bf16[512,1024]{1,0:T(8,128)(2,1)S(1)}, u32[]{:S(2)}, u32[]{:S(2)}) collective-permute-start(bf16[512,1024]{1,0:T(8,128)(2,1)S(1)} %pad_maximum_fusion.yd), channel_id=1, source_target_pairs={{0,12},{4,0},{8,4},{12,8},{1,13},{5,1},{9,5},{13,9},{2,14},{6,2},{... | collective-permute-start | bytes 3145736 | tf_op jit(solution)/shard_map/ppermute | solution.py:25
  114.1 49.5 %collective-permute-start.27 = (bf16[4,128,1024]{2,1,0:T(8,128)(2,1)S(1)}, bf16[4,128,1024]{2,1,0:T(8,128)(2,1)S(1)}, u32[]{:S(2)}, u32[]{:S(2)}) collective-permute-start(bf16[4,128,1024]{2,1,0:T(8,128)(2,1)S(1)} %shard_map.89.bb), channel_id=1, source_target_pairs={{0,16},{16,0},{32,48},{48,32},{64,80},{80,64},{96,112},{112,96},{1... | collective-permute-start | bytes 3145736 | tf_op jit(solution)/shard_map/ppermute | solution.py:314
  118.0 47.9 %collective-permute-start.26 = (bf16[4,128,1024]{2,1,0:T(8,128)(2,1)S(1)}, bf16[4,128,1024]{2,1,0:T(8,128)(2,1)}, u32[]{:S(2)}, u32[]{:S(2)}) collective-permute-start(bf16[4,128,1024]{2,1,0:T(8,128)(2,1)S(1)} %shard_map.88.bt), channel_id=1, source_target_pairs={{0,16},{16,0},{32,48},{48,32},{64,80},{80,64},{96,112},{112,96},{1... | collective-permute-start | bytes 3145736 | tf_op jit(solution)/shard_map/ppermute | solution.py:314
  120.3 18.2 %collective-permute-start.8 = (bf16[384,1024]{1,0:T(8,128)(2,1)S(1)}, bf16[384,1024]{1,0:T(8,128)(2,1)S(1)}, u32[]{:S(2)}, u32[]{:S(2)}) collective-permute-start(bf16[384,1024]{1,0:T(8,128)(2,1)S(1)} %constant_dynamic-update-slice_fusion), channel_id=1, source_target_pairs={{0,1},{1,2},{2,3},{3,0},{4,5},{5,6},{6,7},{7,4},{8,9},{9,10},{10,1... | collective-permute-start | bytes 2359304 | tf_op jit(solution)/shard_map/ppermute | solution.py:24
  120.8 36.4 %collective-permute-start.9 = (bf16[384,1024]{1,0:T(8,128)(2,1)S(1)}, bf16[384,1024]{1,0:T(8,128)(2,1)S(1)}, u32[]{:S(2)}, u32[]{:S(2)}) collective-permute-start(bf16[384,1024]{1,0:T(8,128)(2,1)S(1)} %constant_dynamic-update-slice_fusion), channel_id=1, source_target_pairs={{0,3},{1,0},{2,1},{3,2},{4,7},{5,4},{6,5},{7,6},{8,11},{9,8},{10,9... | collective-permute-start | bytes 2359304 | tf_op jit(solution)/shard_map/ppermute | solution.py:25
  126.5 35.8 %collective-permute-start.7 = (bf16[128,1024]{1,0:T(8,128)(2,1)S(1)}, bf16[128,1024]{1,0:T(8,128)(2,1)S(1)}, u32[]{:S(2)}, u32[]{:S(2)}) collective-permute-start(bf16[128,1024]{1,0:T(8,128)(2,1)S(1)} %add_convert_fusion.1.z0), channel_id=1, source_target_pairs={{0,3},{1,0},{2,1},{3,2},{4,7},{5,4},{6,5},{7,6},{8,11},{9,8},{10,9... | collective-permute-start | bytes 786440 | tf_op jit(solution)/shard_map/ppermute | solution.py:34
  138.5 40.1 %collective-permute-start.31 = (bf16[256,1024]{1,0:T(8,128)(2,1)}, bf16[256,1024]{1,0:T(8,128)(2,1)}, u32[]{:S(2)}, u32[]{:S(2)}) collective-permute-start(bf16[256,1024]{1,0:T(8,128)(2,1)} %slice.18), channel_id=1, source_target_pairs={{0,4},{4,8},{8,12},{12,0},{1,5},{5,9},{9,13},{13,1},{2,6},{6,10},{... | collective-permute-start | bytes 1572872 | tf_op jit(solution)/shard_map/ppermute | solution.py:27
  157.2 21.4 %collective-permute-start.32 = (bf16[256,1024]{1,0:T(8,128)(2,1)}, bf16[256,1024]{1,0:T(8,128)(2,1)}, u32[]{:S(2)}, u32[]{:S(2)}) collective-permute-start(bf16[256,1024]{1,0:T(8,128)(2,1)} %slice.19), channel_id=1, source_target_pairs={{0,12},{4,0},{8,4},{12,8},{1,13},{5,1},{9,5},{13,9},{2,14},{6,2},{... | collective-permute-start | bytes 1572872 | tf_op jit(solution)/shard_map/ppermute | solution.py:28
  162.4 16.2 %collective-permute-start.29 = (bf16[192,1024]{1,0:T(8,128)(2,1)}, bf16[192,1024]{1,0:T(8,128)(2,1)S(1)}, u32[]{:S(2)}, u32[]{:S(2)}) collective-permute-start(bf16[192,1024]{1,0:T(8,128)(2,1)} %slice.16), channel_id=1, source_target_pairs={{0,1},{1,2},{2,3},{3,0},{4,5},{5,6},{6,7},{7,4},{8,9},{9,10},{10,1... | collective-permute-start | bytes 1179656 | tf_op jit(solution)/shard_map/ppermute | solution.py:27
  188.5 18.0 %all-to-all-start = ((f32[16,64,128]{2,1,0:T(8,128)}), f32[16,64,128]{2,1,0:T(8,128)S(1)}, u32[]{:S(2)}, u32[]{:S(2)}) async-start(f32[16,64,128]{2,1,0:T(8,128)} %bitcast.17), calls=%async_computation | async-start | bytes 1048576 | tf_op jit(solution)/shard_map/all_to_all | solution.py:367
  (32 other events, 550.5 us)

commit v2 on v1

--- a/solution.py
+++ b/solution.py
@@ -199,7 +199,7 @@
 
 
 def late_kernel(
-    idx, guess, acc, early, zo, za, zb, ya, yb, bt, bb, ct, cb,
+    idx, guess, zo, za, zb, ya, yb, bt, bb, ct, cb, acc, early,
     updated, applied, z_in, y_in, b_in, part, b_sems, sems,
 ):
     b_copies = columns_in(idx, (bt, bb, ct, cb), b_in, b_sems)
@@ -213,9 +213,14 @@
         pltpu.make_async_copy(ya, y_in.at[:256], sems.at[3]),
         pltpu.make_async_copy(yb.at[:128], y_in.at[256:], sems.at[4]),
     ]
+    kept = [
+        pltpu.make_async_copy(acc, updated, sems.at[6]),
+        pltpu.make_async_copy(early, applied, sems.at[7]),
+    ]
     started(b_copies[3] + z_copies + y_copies)
     for t in range(3):
         started(b_copies[t])
+    started(kept)
     waited(b_copies[3] + z_copies)
     z = dot_t(z_in[...], b_in[3])
     waited(y_copies)
@@ -229,14 +234,13 @@
         part[:512, cols] = z[:512, half]
         part[512:, cols] = y[:, half]
     last = full_dot(part[...], guess[...])
-    updated[...] = acc[...]
-    applied[...] = early[...]
+    waited(kept)
     for i in range(5):
         start = idx[i] if i < 4 else idx[3] + 128
         rows = pl.ds(pl.multiple_of(start, 128), 128)
         mine = slice(128 * i, 128 * i + 128)
-        updated[rows, :] = acc[rows, :] - part[mine, :]
-        applied[rows, :] = early[rows, :] - last[mine]
+        updated[rows, :] = updated[rows, :] - part[mine, :]
+        applied[rows, :] = applied[rows, :] - last[mine]
 
 
 def on_core(kernel, outs, inputs, flops, vmem_mib=24, scratch=(), whole=0):
@@ -350,7 +354,7 @@
     updated, applied = on_core(
         late_kernel,
         (tile, narrow),
-        (idx, guess, acc, early, z_own_far, za, zb, ya, yb, *b_own, *b_other),
+        (idx, guess, z_own_far, za, zb, ya, yb, *b_own, *b_other, acc, early),
         2 * 512 * 1024 * 1024,
         vmem_mib=60,
         scratch=(
@@ -359,9 +363,9 @@
             pltpu.VMEM((4, 512, 1024), BF16),
             pltpu.VMEM((640, 512), F32),
             pltpu.SemaphoreType.DMA((16,)),
-            pltpu.SemaphoreType.DMA((6,)),
+            pltpu.SemaphoreType.DMA((8,)),
         ),
-        whole=9,
+        whole=11,
     )
 
     pieces = lax.all_to_all(applied.reshape(16, 64, R), PLANE, 0, 0, tiled=True)

time: 241 us -> 240 us (level)
  no operation moved by 1% of the time
where the time goes in v2:
time: 240 us
  starting transfers between devices  92.9 us (39%)
  waiting for transfers between devices  87.9 us (37%)
  Pallas kernels  29.7 us (12%)
  blocking collectives  13.1 us (5%)
  local copies, waits for them, and re-layouts  11.5 us (5%)
  between operations  2.91 us (1%)
    ppermute x5, waiting for transfers between devices, gather_direct(): prev = lax.ppermute(block, axis, ring(size, step))  31.3 us
    pallas_call x5, Pallas kernels, on_core(): pl.pallas_call(kernel, out_shape=outs, in_specs=[smem] + [vmem] * (len(in...  24 us
    ppermute x2, starting transfers between devices, gather_ring(): far_a = lax.ppermute(cut_a, axis, ring(size, step))  19.5 us
    ppermute x2, starting transfers between devices, body(): line = lax.ppermute(half, ALL, turned())  15.7 us
    all_to_all x1, blocking collectives, body(): squares = lax.all_to_all(squares, 'row', 0, 0, tiled=True).sum()  13.1 us
    ppermute x5, starting transfers between devices, gather_direct(): succ = lax.ppermute(block, axis, ring(size, -step))  10.9 us
    ppermute x2, waiting for transfers between devices, gather_ring(): prev = lax.ppermute(block, axis, ring(size, step))  10 us
    ppermute x1, waiting for transfers between devices, factor_share(): s_b = lax.ppermute(sb, 'col', ring(4, 1))  9.82 us
  transfers between devices with their start and end apart: 35, of which 16 were waited for; matrix products, arithmetic and copies ran while one was open for 2% of the time, Pallas kernels for 7%

profile of v2, /device:TPU:1, one launch (start us, length us, event | category | flops | bytes accessed | tf_op | source)
XLA Modules:
  0.0 239.8 jit_solution(16963101085528334239)
XLA Ops:
  5.3 4.6 %collective-permute-start.12 = (f32[128,1024]{1,0:T(8,128)S(1)}, f32[128,1024]{1,0:T(8,128)S(1)}, u32[]{:S(2)}, u32[]{:S(2)}) collective-permute-start(f32[128,1024]{1,0:T(8,128)S(1)} %get-tuple-element.26), channel_id=1, source_target_pairs={{0,12},{4,0},{8,4},{12,8},{1,13},{5,1},{9,5},{13,9},{2,14},{6,2},{... | collective-permute-start | bytes 1572872 | tf_op jit(solution)/shard_map/ppermute | solution.py:83
  12.0 8.6 %collective-permute-done.12 = f32[128,1024]{1,0:T(8,128)S(1)} collective-permute-done((f32[128,1024]{1,0:T(8,128)S(1)}, f32[128,1024]{1,0:T(8,128)S(1)}, u32[]{:S(2)}, u32[]{:S(2)}) %collective-permute-start.12) | collective-permute-done | bytes 524320 | tf_op jit(solution)/shard_map/ppermute | solution.py:83
  20.6 3.5 %collective-permute-start.13 = (f32[128,1024]{1,0:T(8,128)S(1)}, f32[128,1024]{1,0:T(8,128)S(1)}, u32[]{:S(2)}, u32[]{:S(2)}) collective-permute-start(f32[128,1024]{1,0:T(8,128)S(1)} %add.146), channel_id=1, source_target_pairs={{0,12},{4,0},{8,4},{12,8},{1,13},{5,1},{9,5},{13,9},{2,14},{6,2},{... | collective-permute-start | bytes 1572872 | tf_op jit(solution)/shard_map/ppermute | solution.py:86
  27.0 9.8 %collective-permute-done.11 = f32[128,1024]{1,0:T(8,128)S(1)} collective-permute-done((f32[128,1024]{1,0:T(8,128)S(1)}, f32[128,1024]{1,0:T(8,128)S(1)}, u32[]{:S(2)}, u32[]{:S(2)}) %collective-permute-start.11) | collective-permute-done | bytes 524320 | tf_op jit(solution)/shard_map/ppermute | solution.py:82
  43.8 12.1 %collective-permute-start.25 = (bf16[128,1024]{1,0:T(8,128)(2,1)S(1)}, bf16[128,1024]{1,0:T(8,128)(2,1)S(1)}, u32[]{:S(2)}, u32[]{:S(2)}) collective-permute-start(bf16[128,1024]{1,0:T(8,128)(2,1)S(1)} %add_convert_fusion), channel_id=1, source_target_pairs={{0,0},{1,32},{2,64},{3,96},{4,16},{5,48},{6,80},{7,112},{8,1},{9,3... | collective-permute-start | bytes 786440 | tf_op jit(solution)/shard_map/ppermute | solution.py:314
  56.3 3.5 %collective-permute-start.21 = (bf16[128,1024]{1,0:T(8,128)(2,1)S(1)}, bf16[128,1024]{1,0:T(8,128)(2,1)S(1)}, u32[]{:S(2)}, u32[]{:S(2)}) collective-permute-start(bf16[128,1024]{1,0:T(8,128)(2,1)S(1)} %add_convert_fusion.1.z0), channel_id=1, source_target_pairs={{0,0},{1,32},{2,64},{3,96},{4,16},{5,48},{6,80},{7,112},{8,1},{9,3... | collective-permute-start | bytes 786440 | tf_op jit(solution)/shard_map/ppermute | solution.py:314
  64.8 6.9 %collective-permute-start.27 = (bf16[128,1024]{1,0:T(8,128)(2,1)S(1)}, bf16[128,1024]{1,0:T(8,128)(2,1)S(1)}, u32[]{:S(2)}, u32[]{:S(2)}) collective-permute-start(bf16[128,1024]{1,0:T(8,128)(2,1)S(1)} %collective-permute-done.25.own), channel_id=1, source_target_pairs={{0,96},{16,112},{32,0},{48,16},{64,32},{80,48},{96,64},{112,80},{1... | collective-permute-start | bytes 786440 | tf_op jit(solution)/shard_map/ppermute | solution.py:34
  71.7 22.1 %collective-permute-done.4.z1 = bf16[128,1024]{1,0:T(8,128)(2,1)S(1)} collective-permute-done((bf16[128,1024]{1,0:T(8,128)(2,1)S(1)}, bf16[128,1024]{1,0:T(8,128)(2,1)S(1)}, u32[]{:S(2)}, u32[]{:S(2)}) %collective-permute-start.4) | collective-permute-done | bytes 262176 | tf_op jit(solution)/shard_map/ppermute | solution.py:33
  93.8 3.2 %collective-permute-start.22 = (bf16[128,1024]{1,0:T(8,128)(2,1)S(1)}, bf16[128,1024]{1,0:T(8,128)(2,1)S(1)}, u32[]{:S(2)}, u32[]{:S(2)}) collective-permute-start(bf16[128,1024]{1,0:T(8,128)(2,1)S(1)} %collective-permute-done.21.own), channel_id=1, source_target_pairs={{0,32},{16,48},{32,64},{48,80},{64,96},{80,112},{96,0},{112,16},{1... | collective-permute-start | bytes 786440 | tf_op jit(solution)/shard_map/ppermute | solution.py:33
  98.9 4.0 %collective-permute-done.28.far = bf16[128,1024]{1,0:T(8,128)(2,1)S(1)} collective-permute-done((bf16[128,1024]{1,0:T(8,128)(2,1)S(1)}, bf16[128,1024]{1,0:T(8,128)(2,1)S(1)}, u32[]{:S(2)}, u32[]{:S(2)}) %collective-permute-start.28) | collective-permute-done | bytes 262176 | tf_op jit(solution)/shard_map/ppermute | solution.py:35
  102.9 6.1 %collective-permute-done.22.prev = bf16[128,1024]{1,0:T(8,128)(2,1)S(1)} collective-permute-done((bf16[128,1024]{1,0:T(8,128)(2,1)S(1)}, bf16[128,1024]{1,0:T(8,128)(2,1)S(1)}, u32[]{:S(2)}, u32[]{:S(2)}) %collective-permute-start.22) | collective-permute-done | bytes 262176 | tf_op jit(solution)/shard_map/ppermute | solution.py:33
  109.0 3.3 %collective-permute-start.6 = (bf16[128,1024]{1,0:T(8,128)(2,1)S(1)}, bf16[128,1024]{1,0:T(8,128)(2,1)S(1)}, u32[]{:S(2)}, u32[]{:S(2)}) collective-permute-start(bf16[128,1024]{1,0:T(8,128)(2,1)S(1)} %add_convert_fusion.1.z0), channel_id=1, source_target_pairs={{0,8},{4,12},{8,0},{12,4},{1,9},{5,13},{9,1},{13,5},{2,10},{6,14},... | collective-permute-start | bytes 786440 | tf_op jit(solution)/shard_map/ppermute | solution.py:35
  123.0 3.6 %collective-permute-done.19.yl = bf16[512,1024]{1,0:T(8,128)(2,1)S(1)} collective-permute-done((bf16[512,1024]{1,0:T(8,128)(2,1)S(1)}, bf16[512,1024]{1,0:T(8,128)(2,1)S(1)}, u32[]{:S(2)}, u32[]{:S(2)}) %collective-permute-start.19) | collective-permute-done | bytes 1048608 | tf_op jit(solution)/shard_map/ppermute | solution.py:25
  128.5 10.0 %collective-permute-done.7.zr = bf16[384,1024]{1,0:T(8,128)(2,1)S(1)} collective-permute-done((bf16[384,1024]{1,0:T(8,128)(2,1)S(1)}, bf16[384,1024]{1,0:T(8,128)(2,1)S(1)}, u32[]{:S(2)}, u32[]{:S(2)}) %collective-permute-start.7) | collective-permute-done | bytes 786464 | tf_op jit(solution)/shard_map/ppermute | solution.py:24
  138.5 18.7 %collective-permute-start.18 = (bf16[256,1024]{1,0:T(8,128)(2,1)}, bf16[256,1024]{1,0:T(8,128)(2,1)}, u32[]{:S(2)}, u32[]{:S(2)}) collective-permute-start(bf16[256,1024]{1,0:T(8,128)(2,1)} %slice.18), channel_id=1, source_target_pairs={{0,4},{4,8},{8,12},{12,0},{1,5},{5,9},{9,13},{13,1},{2,6},{6,10},{... | collective-permute-start | bytes 1572872 | tf_op jit(solution)/shard_map/ppermute | solution.py:27
  157.2 4.3 %collective-permute-start.20 = (bf16[256,1024]{1,0:T(8,128)(2,1)}, bf16[256,1024]{1,0:T(8,128)(2,1)}, u32[]{:S(2)}, u32[]{:S(2)}) collective-permute-start(bf16[256,1024]{1,0:T(8,128)(2,1)} %slice.19), channel_id=1, source_target_pairs={{0,12},{4,0},{8,4},{12,8},{1,13},{5,1},{9,5},{13,9},{2,14},{6,2},{... | collective-permute-start | bytes 1572872 | tf_op jit(solution)/shard_map/ppermute | solution.py:28
  166.7 10.9 %shard_map.90 = (f32[1024,512]{1,0:T(8,128)}, f32[1024,128]{1,0:T(8,128)}) custom-call(s32[11]{0:T(128)} %stack.60.idx, f32[512,128]{1,0:T(8,128)} %guess.3, bf16[128,1024]{1,0:T(8,128)(2,1)} %copy-done.13, bf16[128,1024]{1,0:T(8,128)(2,1)} %copy-done.14, bf16[128,1024]{1,0:T(8,128)(2,1)} %copy-done.15, bf16[128,1024]{1,0:T(8,128)(2,1)} %copy-done.16, ...), custom_call_target="tpu_custom_call" | custom-call | flops 3221225472 | bytes 19136556 | tf_op jit(solution)/shard_map/pallas_call | solution.py:251
  180.2 8.6 %shard_map.91 = (f32[1024,512]{1,0:T(8,128)}, f32[1024,128]{1,0:T(8,128)}) custom-call(s32[11]{0:T(128)} %stack.60.idx, f32[512,128]{1,0:T(8,128)} %guess.3, bf16[128,1024]{1,0:T(8,128)(2,1)} %copy-done.20, bf16[192,1024]{1,0:T(8,128)(2,1)} %copy-done.18, bf16[192,1024]{1,0:T(8,128)(2,1)} %copy-done.17, bf16[256,1024]{1,0:T(8,128)(2,1)} %collective-permute-done.18.ya, ...), custom_call_target="tpu_custom_call" | custom-call | flops 1073741824 | bytes 9175084 | tf_op jit(solution)/shard_map/pallas_call | solution.py:251
  188.8 8.0 %all-to-all-start = ((f32[16,64,128]{2,1,0:T(8,128)}), f32[16,64,128]{2,1,0:T(8,128)S(1)}, u32[]{:S(2)}, u32[]{:S(2)}) async-start(f32[16,64,128]{2,1,0:T(8,128)} %bitcast.17), calls=%async_computation | async-start | bytes 1048576 | tf_op jit(solution)/shard_map/all_to_all | solution.py:371
  196.9 9.6 %all-to-all-done = f32[16,64,128]{2,1,0:T(8,128)S(1)} async-done(((f32[16,64,128]{2,1,0:T(8,128)}), f32[16,64,128]{2,1,0:T(8,128)S(1)}, u32[]{:S(2)}, u32[]{:S(2)}) %all-to-all-start) | async-done | bytes 524320 | tf_op jit(solution)/shard_map/all_to_all | solution.py:371
  208.2 3.8 %all-to-all-start.1 = ((f32[16,64,128]{2,1,0:T(8,128)}), f32[16,64,128]{2,1,0:T(8,128)S(1)}, u32[]{:S(2)}, u32[]{:S(2)}) async-start(f32[16,64,128]{2,1,0:T(8,128)} %broadcast_in_dim.2), calls=%async_computation.1 | async-start | bytes 1048576 | tf_op jit(solution)/shard_map/all_to_all | solution.py:374
  212.0 3.5 %shard_map.92.gram = f32[2,512,512]{2,1,0:T(8,128)S(1)} custom-call(f32[1024,512]{1,0:T(8,128)S(1)} %copy-done.4), custom_call_target="tpu_custom_call" | custom-call | flops 4294967296 | bytes 4194304 | tf_op jit(solution)/shard_map/pallas_call | solution.py:305
  216.8 3.9 %all-to-all-done.1 = f32[16,64,128]{2,1,0:T(8,128)S(1)} async-done(((f32[16,64,128]{2,1,0:T(8,128)}), f32[16,64,128]{2,1,0:T(8,128)S(1)}, u32[]{:S(2)}, u32[]{:S(2)}) %all-to-all-start.1) | async-done | bytes 524320 | tf_op jit(solution)/shard_map/all_to_all | solution.py:374
  224.3 13.1 %all_to_all.15 = f32[8,8,128]{2,1,0:T(8,128)S(1)} all-to-all(f32[8,8,128]{2,1,0:T(8,128)S(1)} %get-tuple-element.32), channel_id=1, replica_groups=mesh['row'=8,'col'=4,'depth'=4] {'row'}, dimensions={0} | all-to-all | bytes 65536 | tf_op jit(solution)/shard_map/all_to_all | solution.py:382
  (116 shorter events, 51.1 us)
Async XLA Ops:
  11.9 25.0 %collective-permute-start.11 = (f32[128,1024]{1,0:T(8,128)S(1)}, f32[128,1024]{1,0:T(8,128)S(1)}, u32[]{:S(2)}, u32[]{:S(2)}) collective-permute-start(f32[128,1024]{1,0:T(8,128)S(1)} %get-tuple-element.24), channel_id=1, source_target_pairs={{0,4},{4,8},{8,12},{12,0},{1,5},{5,9},{9,13},{13,1},{2,6},{6,10},{... | collective-permute-start | bytes 1572872 | tf_op jit(solution)/shard_map/ppermute | solution.py:82
  20.6 16.2 %collective-permute-start.13 = (f32[128,1024]{1,0:T(8,128)S(1)}, f32[128,1024]{1,0:T(8,128)S(1)}, u32[]{:S(2)}, u32[]{:S(2)}) collective-permute-start(f32[128,1024]{1,0:T(8,128)S(1)} %add.146), channel_id=1, source_target_pairs={{0,12},{4,0},{8,4},{12,8},{1,13},{5,1},{9,5},{13,9},{2,14},{6,2},{... | collective-permute-start | bytes 1572872 | tf_op jit(solution)/shard_map/ppermute | solution.py:86
  24.1 32.0 %collective-permute-start.2 = (f32[128,1024]{1,0:T(8,128)S(1)}, f32[128,1024]{1,0:T(8,128)S(1)}, u32[]{:S(2)}, u32[]{:S(2)}) collective-permute-start(f32[128,1024]{1,0:T(8,128)S(1)} %get-tuple-element.22), channel_id=1, source_target_pairs={{0,12},{4,0},{8,4},{12,8},{1,13},{5,1},{9,5},{13,9},{2,14},{6,2},{... | collective-permute-start | bytes 1572872 | tf_op jit(solution)/shard_map/ppermute | solution.py:87
  25.7 30.5 %collective-permute-start.1 = (f32[128,1024]{1,0:T(8,128)S(1)}, f32[128,1024]{1,0:T(8,128)S(1)}, u32[]{:S(2)}, u32[]{:S(2)}) collective-permute-start(f32[128,1024]{1,0:T(8,128)S(1)} %add.142), channel_id=1, source_target_pairs={{0,4},{4,8},{8,12},{12,0},{1,5},{5,9},{9,13},{13,1},{2,6},{6,10},{... | collective-permute-start | bytes 1572872 | tf_op jit(solution)/shard_map/ppermute | solution.py:88
  38.3 17.6 %collective-permute-start.15 = (bf16[128,1024]{1,0:T(8,128)(2,1)S(1)}, bf16[128,1024]{1,0:T(8,128)(2,1)S(1)}, u32[]{:S(2)}, u32[]{:S(2)}) collective-permute-start(bf16[128,1024]{1,0:T(8,128)(2,1)S(1)} %add_convert_fusion), channel_id=1, source_target_pairs={{0,3},{1,0},{2,1},{3,2},{4,7},{5,4},{6,5},{7,6},{8,11},{9,8},{10,9... | collective-permute-start | bytes 786440 | tf_op jit(solution)/shard_map/ppermute | solution.py:34
  39.8 16.1 %collective-permute-start.16 = (bf16[128,1024]{1,0:T(8,128)(2,1)S(1)}, bf16[128,1024]{1,0:T(8,128)(2,1)S(1)}, u32[]{:S(2)}, u32[]{:S(2)}) collective-permute-start(bf16[128,1024]{1,0:T(8,128)(2,1)S(1)} %add_convert_fusion), channel_id=1, source_target_pairs={{0,2},{1,3},{2,0},{3,1},{4,6},{5,7},{6,4},{7,5},{8,10},{9,11},{10,... | collective-permute-start | bytes 786440 | tf_op jit(solution)/shard_map/ppermute | solution.py:35
  43.8 18.8 %collective-permute-start.25 = (bf16[128,1024]{1,0:T(8,128)(2,1)S(1)}, bf16[128,1024]{1,0:T(8,128)(2,1)S(1)}, u32[]{:S(2)}, u32[]{:S(2)}) collective-permute-start(bf16[128,1024]{1,0:T(8,128)(2,1)S(1)} %add_convert_fusion), channel_id=1, source_target_pairs={{0,0},{1,32},{2,64},{3,96},{4,16},{5,48},{6,80},{7,112},{8,1},{9,3... | collective-permute-start | bytes 786440 | tf_op jit(solution)/shard_map/ppermute | solution.py:314
  56.0 64.8 %collective-permute-start.17 = (bf16[512,1024]{1,0:T(8,128)(2,1)S(1)}, bf16[512,1024]{1,0:T(8,128)(2,1)S(1)}, u32[]{:S(2)}, u32[]{:S(2)}) collective-permute-start(bf16[512,1024]{1,0:T(8,128)(2,1)S(1)} %pad_maximum_fusion.yd), channel_id=1, source_target_pairs={{0,4},{4,8},{8,12},{12,0},{1,5},{5,9},{9,13},{13,1},{2,6},{6,10},{... | collective-permute-start | bytes 3145736 | tf_op jit(solution)/shard_map/ppermute | solution.py:24
  59.8 34.0 %collective-permute-start.4 = (bf16[128,1024]{1,0:T(8,128)(2,1)S(1)}, bf16[128,1024]{1,0:T(8,128)(2,1)S(1)}, u32[]{:S(2)}, u32[]{:S(2)}) collective-permute-start(bf16[128,1024]{1,0:T(8,128)(2,1)S(1)} %add_convert_fusion.1.z0), channel_id=1, source_target_pairs={{0,4},{4,8},{8,12},{12,0},{1,5},{5,9},{9,13},{13,1},{2,6},{6,10},{... | collective-permute-start | bytes 786440 | tf_op jit(solution)/shard_map/ppermute | solution.py:33
  60.2 33.6 %collective-permute-start.5 = (bf16[128,1024]{1,0:T(8,128)(2,1)S(1)}, bf16[128,1024]{1,0:T(8,128)(2,1)S(1)}, u32[]{:S(2)}, u32[]{:S(2)}) collective-permute-start(bf16[128,1024]{1,0:T(8,128)(2,1)S(1)} %add_convert_fusion.1.z0), channel_id=1, source_target_pairs={{0,12},{4,0},{8,4},{12,8},{1,13},{5,1},{9,5},{13,9},{2,14},{6,2},{... | collective-permute-start | bytes 786440 | tf_op jit(solution)/shard_map/ppermute | solution.py:34
  62.6 34.5 %collective-permute-start.26 = (bf16[128,1024]{1,0:T(8,128)(2,1)S(1)}, bf16[128,1024]{1,0:T(8,128)(2,1)S(1)}, u32[]{:S(2)}, u32[]{:S(2)}) collective-permute-start(bf16[128,1024]{1,0:T(8,128)(2,1)S(1)} %collective-permute-done.25.own), channel_id=1, source_target_pairs={{0,32},{16,48},{32,64},{48,80},{64,96},{80,112},{96,0},{112,16},{1... | collective-permute-start | bytes 786440 | tf_op jit(solution)/shard_map/ppermute | solution.py:33
  64.8 32.3 %collective-permute-start.27 = (bf16[128,1024]{1,0:T(8,128)(2,1)S(1)}, bf16[128,1024]{1,0:T(8,128)(2,1)S(1)}, u32[]{:S(2)}, u32[]{:S(2)}) collective-permute-start(bf16[128,1024]{1,0:T(8,128)(2,1)S(1)} %collective-permute-done.25.own), channel_id=1, source_target_pairs={{0,96},{16,112},{32,0},{48,16},{64,32},{80,48},{96,64},{112,80},{1... | collective-permute-start | bytes 786440 | tf_op jit(solution)/shard_map/ppermute | solution.py:34
  97.0 17.1 %collective-permute-start.24 = (bf16[128,1024]{1,0:T(8,128)(2,1)S(1)}, bf16[128,1024]{1,0:T(8,128)(2,1)S(1)}, u32[]{:S(2)}, u32[]{:S(2)}) collective-permute-start(bf16[128,1024]{1,0:T(8,128)(2,1)S(1)} %collective-permute-done.21.own), channel_id=1, source_target_pairs={{0,64},{16,80},{32,96},{48,112},{64,0},{80,16},{96,32},{112,48},{1... | collective-permute-start | bytes 786440 | tf_op jit(solution)/shard_map/ppermute | solution.py:35
  102.9 23.6 %collective-permute-start.19 = (bf16[512,1024]{1,0:T(8,128)(2,1)S(1)}, bf16[512,1024]{1,0:T(8,128)(2,1)S(1)}, u32[]{:S(2)}, u32[]{:S(2)}) collective-permute-start(bf16[512,1024]{1,0:T(8,128)(2,1)S(1)} %pad_maximum_fusion.yd), channel_id=1, source_target_pairs={{0,12},{4,0},{8,4},{12,8},{1,13},{5,1},{9,5},{13,9},{2,14},{6,2},{... | collective-permute-start | bytes 3145736 | tf_op jit(solution)/shard_map/ppermute | solution.py:25
  114.1 49.3 %collective-permute-start.30 = (bf16[4,128,1024]{2,1,0:T(8,128)(2,1)S(1)}, bf16[4,128,1024]{2,1,0:T(8,128)(2,1)S(1)}, u32[]{:S(2)}, u32[]{:S(2)}) collective-permute-start(bf16[4,128,1024]{2,1,0:T(8,128)(2,1)S(1)} %shard_map.89.bb), channel_id=1, source_target_pairs={{0,16},{16,0},{32,48},{48,32},{64,80},{80,64},{96,112},{112,96},{1... | collective-permute-start | bytes 3145736 | tf_op jit(solution)/shard_map/ppermute | solution.py:318
  118.0 46.9 %collective-permute-start.29 = (bf16[4,128,1024]{2,1,0:T(8,128)(2,1)S(1)}, bf16[4,128,1024]{2,1,0:T(8,128)(2,1)}, u32[]{:S(2)}, u32[]{:S(2)}) collective-permute-start(bf16[4,128,1024]{2,1,0:T(8,128)(2,1)S(1)} %shard_map.88.bt), channel_id=1, source_target_pairs={{0,16},{16,0},{32,48},{48,32},{64,80},{80,64},{96,112},{112,96},{1... | collective-permute-start | bytes 3145736 | tf_op jit(solution)/shard_map/ppermute | solution.py:318
  120.3 18.2 %collective-permute-start.7 = (bf16[384,1024]{1,0:T(8,128)(2,1)S(1)}, bf16[384,1024]{1,0:T(8,128)(2,1)S(1)}, u32[]{:S(2)}, u32[]{:S(2)}) collective-permute-start(bf16[384,1024]{1,0:T(8,128)(2,1)S(1)} %constant_dynamic-update-slice_fusion), channel_id=1, source_target_pairs={{0,1},{1,2},{2,3},{3,0},{4,5},{5,6},{6,7},{7,4},{8,9},{9,10},{10,1... | collective-permute-start | bytes 2359304 | tf_op jit(solution)/shard_map/ppermute | solution.py:24
  120.8 36.4 %collective-permute-start.9 = (bf16[384,1024]{1,0:T(8,128)(2,1)S(1)}, bf16[384,1024]{1,0:T(8,128)(2,1)S(1)}, u32[]{:S(2)}, u32[]{:S(2)}) collective-permute-start(bf16[384,1024]{1,0:T(8,128)(2,1)S(1)} %constant_dynamic-update-slice_fusion), channel_id=1, source_target_pairs={{0,3},{1,0},{2,1},{3,2},{4,7},{5,4},{6,5},{7,6},{8,11},{9,8},{10,9... | collective-permute-start | bytes 2359304 | tf_op jit(solution)/shard_map/ppermute | solution.py:25
  126.5 35.8 %collective-permute-start.32 = (bf16[128,1024]{1,0:T(8,128)(2,1)S(1)}, bf16[128,1024]{1,0:T(8,128)(2,1)S(1)}, u32[]{:S(2)}, u32[]{:S(2)}) collective-permute-start(bf16[128,1024]{1,0:T(8,128)(2,1)S(1)} %add_convert_fusion.1.z0), channel_id=1, source_target_pairs={{0,3},{1,0},{2,1},{3,2},{4,7},{5,4},{6,5},{7,6},{8,11},{9,8},{10,9... | collective-permute-start | bytes 786440 | tf_op jit(solution)/shard_map/ppermute | solution.py:34
  138.5 40.7 %collective-permute-start.18 = (bf16[256,1024]{1,0:T(8,128)(2,1)}, bf16[256,1024]{1,0:T(8,128)(2,1)}, u32[]{:S(2)}, u32[]{:S(2)}) collective-permute-start(bf16[256,1024]{1,0:T(8,128)(2,1)} %slice.18), channel_id=1, source_target_pairs={{0,4},{4,8},{8,12},{12,0},{1,5},{5,9},{9,13},{13,1},{2,6},{6,10},{... | collective-permute-start | bytes 1572872 | tf_op jit(solution)/shard_map/ppermute | solution.py:27
  157.2 22.0 %collective-permute-start.20 = (bf16[256,1024]{1,0:T(8,128)(2,1)}, bf16[256,1024]{1,0:T(8,128)(2,1)}, u32[]{:S(2)}, u32[]{:S(2)}) collective-permute-start(bf16[256,1024]{1,0:T(8,128)(2,1)} %slice.19), channel_id=1, source_target_pairs={{0,12},{4,0},{8,4},{12,8},{1,13},{5,1},{9,5},{13,9},{2,14},{6,2},{... | collective-permute-start | bytes 1572872 | tf_op jit(solution)/shard_map/ppermute | solution.py:28
  162.4 16.8 %collective-permute-start.10 = (bf16[192,1024]{1,0:T(8,128)(2,1)}, bf16[192,1024]{1,0:T(8,128)(2,1)S(1)}, u32[]{:S(2)}, u32[]{:S(2)}) collective-permute-start(bf16[192,1024]{1,0:T(8,128)(2,1)} %slice.17), channel_id=1, source_target_pairs={{0,3},{1,0},{2,1},{3,2},{4,7},{5,4},{6,5},{7,6},{8,11},{9,8},{10,9... | collective-permute-start | bytes 1179656 | tf_op jit(solution)/shard_map/ppermute | solution.py:28
  163.5 15.7 %collective-permute-start.8 = (bf16[192,1024]{1,0:T(8,128)(2,1)S(1)}, bf16[192,1024]{1,0:T(8,128)(2,1)S(1)}, u32[]{:S(2)}, u32[]{:S(2)}) collective-permute-start(bf16[192,1024]{1,0:T(8,128)(2,1)S(1)} %slice.16), channel_id=1, source_target_pairs={{0,1},{1,2},{2,3},{3,0},{4,5},{5,6},{6,7},{7,4},{8,9},{9,10},{10,1... | collective-permute-start | bytes 1179656 | tf_op jit(solution)/shard_map/ppermute | solution.py:27
  188.8 17.7 %all-to-all-start = ((f32[16,64,128]{2,1,0:T(8,128)}), f32[16,64,128]{2,1,0:T(8,128)S(1)}, u32[]{:S(2)}, u32[]{:S(2)}) async-start(f32[16,64,128]{2,1,0:T(8,128)} %bitcast.17), calls=%async_computation | async-start | bytes 1048576 | tf_op jit(solution)/shard_map/all_to_all | solution.py:371
  (32 other events, 549.1 us)
